TPU v7x, 32 devices: a whole 2x2x4 slice. The times are simulated.
32 devices in a mesh: rows: 8 (over z, x), cols: 4 (over y, core).
Axes of the slice: x: 2, y: 2, z: 4, core: 2. Of those that a mesh axis runs over, the one named last changes fastest.
Arguments:
- leading_scene_data: float32 [2, 1024, 8192], P(None, 'rows', 'cols'), may hold values from -12 to 12, as said below
- trailing_scene_data: float32 [2, 1024, 8192], P(None, 'rows', 'cols'), may hold values from -20 to 20, as said below
- shared_usable_flags: int32 [1024, 8192], P('rows', 'cols'), may hold values 0 or 1
- sweep_of_each_line: int32 [1024], P('rows'), may hold values from 0 to 15, never falling along the last dimension, each value on 1 to 128 neighbouring positions
Outputs:
- deramped: float32 [2, 1024, 8192], P(None, 'rows', 'cols')
- coherence: float32 [1024, 8192], P('rows', 'cols')
Inputs may be any that keep to these rules, and one draw needn't show every extreme that they name: `leading_scene_data`: first scene's parts lie in [-12, 12]. `trailing_scene_data`: second scene's parts lie in [-20, 20]; it is the first scene rotated by a smooth phase plus independent noise. `sweep_of_each_line`: burst ids never fall along the rows; each burst holds 1 to 128 rows, one exactly that many.
All inputs are finite; a program needn't handle non-finite values.
Results may differ from a plain program's by a relative error of at most 0.0003.
Values sent between devices are 32-bit elements.
A program may use at most 64 MiB of HBM per device.

v0:
```python
import functools

import jax
import jax.numpy as jnp
from jax import lax
from jax.experimental import pallas as pl
from jax.experimental.pallas import tpu as pltpu
from jax.sharding import PartitionSpec as P

WIN_R = 32
WIN_C = 8
SWEEP_TALLY = 16

EDGE = WIN_R // 2
SIDE = WIN_C // 2
LANES = 128
SCALE = 2.0**56
FLOOR = 1e-36
F32 = jnp.float32
BF16 = jnp.bfloat16
MESH = pl.DeviceIdType.MESH


def masked(av, bv, wv, rows, lanes):
    w = wv[rows, lanes].astype(F32)
    return av[0, rows, lanes] * w, av[1, rows, lanes] * w, bv[0, rows, lanes] * w, bv[1, rows, lanes] * w


def encode(ar, ai, br, bi):
    sr, si = ar * SCALE, ai * SCALE
    power = sr * sr + si * si
    some = power > FLOOR
    inverse = lax.rsqrt(jnp.where(some, power, 1.0))
    return (
        jnp.where(some, power * inverse * (1.0 / SCALE), 0.0),
        jnp.where(some, (sr * br + si * bi) * inverse, br),
        jnp.where(some, (si * br - sr * bi) * inverse, bi),
    )


def decode(s, gr, gi):
    return s * gr, s * gi, s * s, gr * gr + gi * gi


def put_split(out, products, lanes, rows, low_rows):
    for plane, value in enumerate(products):
        high = value.astype(BF16)
        out[plane, rows, lanes] = high
        out[plane, low_rows, lanes] = (value - high.astype(F32)).astype(BF16)


def edge_block(pack):
    lane = lax.broadcasted_iota(jnp.int32, pack.shape, 1)
    left, right = lane >= LANES - SIDE, lane < SIDE

    def pick(k):
        a = pack if k == 0 else pltpu.roll(pack, k * SIDE, 1)
        b = pack if k == 0 else pltpu.roll(pack, LANES - k * SIDE, 1)
        return jnp.where(left, a, jnp.where(right, b, 0.0))

    return pick(0), pick(1), pick(2)


def front_kernel(
    n_rows, n_cols,
    lead, trail, flags, sweep,
    gam, coef, across,
    av, bv, wv, up_out, down_out, top_in, bot_in, left_out, right_out, left_in, right_in,
    corner, corner_top, corner_bot, split, halo_split, vert, lines, member,
    tab_out, tab_cols, sum_out, tab_rows,
    load_sem, halo_send, halo_recv, side_send, side_recv, corner_send, corner_recv,
    cols_send, cols_recv, rows_send, rows_recv,
):
    me_r, me_c = lax.axis_index("rows"), lax.axis_index("cols")
    height, width = flags.shape
    wide = width + LANES
    low = height - EDGE
    chunk = 512 if width % 512 == 0 else LANES
    has_up, has_down = me_r > 0, me_r < n_rows - 1
    has_left, has_right = me_c > 0, me_c < n_cols - 1

    loads = []
    for part, (first, count) in enumerate(((low, EDGE), (0, EDGE), (EDGE, low - EDGE))):
        rows = pl.ds(first, count)
        group = [
            pltpu.make_async_copy(lead.at[:, rows, :], av.at[:, rows, :], load_sem.at[part, 0]),
            pltpu.make_async_copy(trail.at[:, rows, :], bv.at[:, rows, :], load_sem.at[part, 1]),
            pltpu.make_async_copy(flags.at[rows, :], wv.at[rows, :], load_sem.at[part, 2]),
        ]
        for copy in group:
            copy.start()
        loads.append(group)

    barrier = pltpu.get_barrier_semaphore()
    for k in range(1, n_rows):
        pl.semaphore_signal(barrier, inc=1, device_id=(lax.rem(me_r + k, n_rows), me_c), device_id_type=MESH)
    for k in range(1, n_cols):
        pl.semaphore_signal(barrier, inc=1, device_id=(me_r, lax.rem(me_c + k, n_cols)), device_id_type=MESH)

    def remote(src, dst, send, recv, row, col):
        return pltpu.make_async_remote_copy(
            src_ref=src, dst_ref=dst, send_sem=send, recv_sem=recv, device_id=(row, col), device_id_type=MESH
        )

    down = remote(down_out, top_in, halo_send.at[0], halo_recv.at[0], me_r + 1, me_c)
    up = remote(up_out, bot_in, halo_send.at[1], halo_recv.at[1], me_r - 1, me_c)
    to_right = remote(right_out, left_in, side_send.at[0], side_recv.at[0], me_r, me_c + 1)
    to_left = remote(left_out, right_in, side_send.at[1], side_recv.at[1], me_r, me_c - 1)
    corner_down = remote(
        corner.at[pl.ds(low, EDGE)], corner_top, corner_send.at[0], corner_recv.at[0], me_r + 1, me_c
    )
    corner_up = remote(
        corner.at[pl.ds(0, EDGE)], corner_bot, corner_send.at[1], corner_recv.at[1], me_r - 1, me_c
    )

    def encode_rows(first, out):
        @pl.loop(0, width // chunk)
        def _(c):
            lanes = pl.ds(pl.multiple_of(c * chunk, chunk), chunk)
            for k, value in enumerate(encode(*masked(av, bv, wv, pl.ds(first, EDGE), lanes))):
                out[k, :, lanes] = value

    for copy in loads[0]:
        copy.wait()
    encode_rows(low, down_out)
    for copy in loads[1]:
        copy.wait()
    encode_rows(0, up_out)

    pl.semaphore_wait(barrier, n_rows - 1 + n_cols - 1)

    @pl.when(has_down)
    def _():
        down.start()

    @pl.when(has_up)
    def _():
        up.start()

    for copy in loads[2]:
        copy.wait()

    @pl.loop(0, height // 16)
    def _(b):
        rows = pl.ds(pl.multiple_of(b * 16, 16), 16)
        lane = lax.broadcasted_iota(jnp.int32, (16, LANES), 1)
        s, gr, gi = encode(*masked(av, bv, wv, rows, pl.ds(width - LANES, LANES)))
        right_out[rows, :] = jnp.where(
            lane >= LANES - SIDE,
            s,
            jnp.where(
                lane >= LANES - 2 * SIDE,
                pltpu.roll(gr, LANES - SIDE, 1),
                jnp.where(lane >= LANES - 3 * SIDE, pltpu.roll(gi, LANES - 2 * SIDE, 1), 0.0),
            ),
        )
        s, gr, gi = encode(*masked(av, bv, wv, rows, pl.ds(0, LANES)))
        left_out[rows, :] = jnp.where(
            lane < SIDE,
            s,
            jnp.where(
                lane < 2 * SIDE,
                pltpu.roll(gr, SIDE, 1),
                jnp.where(lane < 3 * SIDE, pltpu.roll(gi, 2 * SIDE, 1), 0.0),
            ),
        )

    @pl.when(jnp.logical_not(has_left))
    def _():
        left_in[...] = jnp.zeros_like(left_in)

    @pl.when(jnp.logical_not(has_right))
    def _():
        right_in[...] = jnp.zeros_like(right_in)

    @pl.when(jnp.logical_not(has_up))
    def _():
        top_in[...] = jnp.zeros_like(top_in)
        corner_top[...] = jnp.zeros_like(corner_top)

    @pl.when(jnp.logical_not(has_down))
    def _():
        bot_in[...] = jnp.zeros_like(bot_in)
        corner_bot[...] = jnp.zeros_like(corner_bot)

    @pl.when(has_right)
    def _():
        to_right.start()

    @pl.when(has_left)
    def _():
        to_left.start()

    @pl.loop(0, height // 16)
    def _(b):
        rows = pl.ds(pl.multiple_of(b * 16, 16), 16)
        low_rows = pl.ds(pl.multiple_of(height + b * 16, 16), 16)

        @pl.loop(0, width // chunk)
        def _(c):
            lanes = pl.ds(pl.multiple_of(c * chunk, chunk), chunk)
            ar, ai, br, bi = masked(av, bv, wv, rows, lanes)
            put_split(
                split,
                (ar * br + ai * bi, ai * br - ar * bi, ar * ar + ai * ai, br * br + bi * bi),
                lanes, rows, low_rows,
            )

    total_rows, total_cols = height * n_rows, width * n_cols
    lane_all = lax.broadcasted_iota(jnp.int32, (8, width), 1) + me_c * width
    across[...] = (lane_all.astype(F32) + 0.5) * (2.0 / total_cols) - 1.0
    member[...] = (lax.broadcasted_iota(jnp.int32, (LANES, height), 0) == sweep[...]).astype(F32)

    @pl.when(has_left)
    def _():
        to_right_wait = to_right
        to_right_wait.wait_recv()

    @pl.when(has_right)
    def _():
        to_left.wait_recv()

    @pl.loop(0, height // 16)
    def _(b):
        rows = pl.ds(pl.multiple_of(b * 16, 16), 16)
        low_rows = pl.ds(pl.multiple_of(height + b * 16, 16), 16)
        lane = lax.broadcasted_iota(jnp.int32, (16, LANES), 1)
        pack = jnp.where(lane >= LANES // 2, left_in[rows, :], right_in[rows, :])
        corner[rows, :] = pack
        put_split(split, decode(*edge_block(pack)), pl.ds(width, LANES), rows, low_rows)

    r = lax.broadcasted_iota(jnp.int32, (height, 2 * height), 0)
    k = lax.rem(lax.broadcasted_iota(jnp.int32, (height, 2 * height), 1), height)
    band = jnp.logical_and(k >= r - EDGE, k < r + EDGE).astype(F32).astype(BF16)

    @pl.loop(0, wide // LANES)
    def _(c):
        lanes = pl.ds(pl.multiple_of(c * LANES, LANES), LANES)
        for plane in range(4):
            vert[plane, :, lanes] = jnp.dot(band, split[plane, :, lanes], preferred_element_type=F32)

    @pl.when(has_down)
    def _():
        corner_down.start()

    @pl.when(has_up)
    def _():
        corner_up.start()

    def finish(first):
        rows = pl.ds(first, 8)

        def across_sum(plane):
            x = vert[plane, rows, :]
            x = x + pltpu.roll(x, wide - 1, 1)
            x = x + pltpu.roll(x, wide - 2, 1)
            return x + pltpu.roll(x, wide - 4, 1)

        inverse = lax.rsqrt((across_sum(2) + 1.0) * (across_sum(3) + 1.0))
        real = pltpu.roll(across_sum(0) * inverse, SIDE, 1)[:, :width]
        imag = pltpu.roll(across_sum(1) * inverse, SIDE, 1)[:, :width]
        gam[0, rows, :] = real
        gam[1, rows, :] = imag
        u = across[...]
        w = wv[rows, :].astype(F32)
        wu = w * u
        s0 = jnp.sum(w, 1, keepdims=True)
        su = jnp.sum(wu, 1, keepdims=True)
        suu = jnp.sum(wu * u, 1, keepdims=True)
        hr = jnp.sum(w * real, 1, keepdims=True)
        hi = jnp.sum(w * imag, 1, keepdims=True)
        hur = jnp.sum(wu * real, 1, keepdims=True)
        hui = jnp.sum(wu * imag, 1, keepdims=True)
        row = lax.broadcasted_iota(jnp.int32, (8, 1), 0) + (me_r * height + first)
        v = (row.astype(F32) + 0.5) * (2.0 / total_rows) - 1.0
        lane = lax.broadcasted_iota(jnp.int32, (8, LANES), 1)
        table = jnp.zeros((8, LANES), F32)
        for m, value in enumerate((s0, su, v * s0, suu, v * su, v * v * s0, hr, hi, hur, hui, v * hr, v * hi)):
            table = jnp.where(lane == m, value, table)
        lines[rows, :] = table

    @pl.loop(0, (low - EDGE) // 8)
    def _(b):
        finish(pl.multiple_of(EDGE + b * 8, 8))

    @pl.when(has_up)
    def _():
        down.wait_recv()

    @pl.when(has_down)
    def _():
        up.wait_recv()

    for part, halo in enumerate((top_in, bot_in)):
        rows = pl.ds(2 * part * EDGE, EDGE)
        low_rows = pl.ds((2 * part + 1) * EDGE, EDGE)

        @pl.loop(0, width // chunk)
        def _(c):
            lanes = pl.ds(pl.multiple_of(c * chunk, chunk), chunk)
            put_split(
                halo_split, decode(halo[0, :, lanes], halo[1, :, lanes], halo[2, :, lanes]), lanes, rows, low_rows
            )

    @pl.when(has_up)
    def _():
        corner_down.wait_recv()

    @pl.when(has_down)
    def _():
        corner_up.wait_recv()

    for part, pack in enumerate((corner_top, corner_bot)):
        put_split(
            halo_split, decode(*edge_block(pack[...])), pl.ds(width, LANES),
            pl.ds(2 * part * EDGE, EDGE), pl.ds((2 * part + 1) * EDGE, EDGE),
        )

    r = lax.broadcasted_iota(jnp.int32, (2 * EDGE, 4 * EDGE), 0)
    k = lax.broadcasted_iota(jnp.int32, (2 * EDGE, 4 * EDGE), 1)
    within = lax.rem(k, EDGE)
    upper = jnp.logical_and(jnp.logical_and(r < EDGE, k < 2 * EDGE), within >= r)
    lower = jnp.logical_and(jnp.logical_and(r >= EDGE, k >= 2 * EDGE), within < r - EDGE)
    reach = jnp.logical_or(upper, lower).astype(F32).astype(BF16)

    for plane in range(4):
        extra = jnp.dot(reach, halo_split[plane], preferred_element_type=F32)
        vert[plane, 0:EDGE, :] += extra[:EDGE]
        vert[plane, low:height, :] += extra[EDGE:]

    @pl.loop(0, 2 * EDGE // 8)
    def _(b):
        finish(pl.multiple_of(b * 8 + (b // (EDGE // 8)) * (low - EDGE), 8))

    exact = lax.Precision.HIGHEST
    tab_out[...] = jnp.dot(
        member[0:SWEEP_TALLY, :], lines[...], preferred_element_type=F32, precision=exact
    )
    swaps = [
        remote(tab_out, tab_cols.at[k - 1], cols_send.at[k - 1], cols_recv.at[k - 1], me_r, lax.rem(me_c + k, n_cols))
        for k in range(1, n_cols)
    ]
    for copy in swaps:
        copy.start()
    for copy in swaps:
        copy.wait_recv()
    total = tab_out[...]
    for k in range(n_cols - 1):
        total = total + tab_cols[k]
    sum_out[...] = total
    tours = [
        remote(sum_out, tab_rows.at[k - 1], rows_send.at[k - 1], rows_recv.at[k - 1], lax.rem(me_r + k, n_rows), me_c)
        for k in range(1, n_rows)
    ]
    for copy in tours:
        copy.start()
    for copy in tours:
        copy.wait_recv()
    for k in range(n_rows - 1):
        total = total + tab_rows[k]

    def column(m):
        return total[:, m : m + 1]

    s0, su, sv, suu, suv, svv, hr, hi, hur, hui, hvr, hvi = [column(m) for m in range(12)]
    floored = jnp.maximum(s0, 1.0)
    mid_u, mid_v = su / floored, sv / floored
    guu = suu - 2.0 * mid_u * su + mid_u * mid_u * s0
    guv = suv - mid_u * sv - mid_v * su + mid_u * mid_v * s0
    gvv = svv - 2.0 * mid_v * sv + mid_v * mid_v * s0
    hur, hui = hur - mid_u * hr, hui - mid_u * hi
    hvr, hvi = hvr - mid_v * hr, hvi - mid_v * hi
    ridge = 0.001 * s0 + 1.0
    duu, dvv = guu + ridge, gvv + ridge
    scale = 1.0 / (duu * dvv - guv * guv)
    base = 1.0 / (s0 + ridge)
    fits = (
        mid_u, mid_v, hr * base, hi * base,
        (dvv * hur - guv * hvr) * scale, (dvv * hui - guv * hvi) * scale,
        (duu * hvr - guv * hur) * scale, (duu * hvi - guv * hui) * scale,
    )
    lane = lax.broadcasted_iota(jnp.int32, (SWEEP_TALLY, LANES), 1)
    fit_table = jnp.zeros((SWEEP_TALLY, LANES), F32)
    for m, value in enumerate(fits):
        fit_table = jnp.where(lane == m, value, fit_table)
    spread = jnp.concatenate([fit_table, jnp.zeros((LANES - SWEEP_TALLY, LANES), F32)], 0)
    coef[...] = jnp.dot(member[...].T, spread, preferred_element_type=F32, precision=exact)

    @pl.when(has_down)
    def _():
        down.wait_send()
        corner_down.wait_send()

    @pl.when(has_up)
    def _():
        up.wait_send()
        corner_up.wait_send()

    @pl.when(has_right)
    def _():
        to_right.wait_send()

    @pl.when(has_left)
    def _():
        to_left.wait_send()

    for copy in swaps + tours:
        copy.wait_send()


def back_kernel(n_rows, block, gam, coef, across, ramped, coherence):
    height = gam.shape[1]
    step = pl.program_id(0)
    me_r = lax.axis_index("rows")

    @pl.loop(0, block // 8)
    def _(b):
        inner = pl.ds(pl.multiple_of(b * 8, 8), 8)
        first = pl.multiple_of(step * block + b * 8, 8)
        rows = pl.ds(first, 8)
        line = coef[rows, :]
        row = lax.broadcasted_iota(jnp.int32, (8, 1), 0) + (me_r * height + first)
        v = (row.astype(F32) + 0.5) * (2.0 / (height * n_rows)) - 1.0
        dv = v - line[:, 1:2]
        real, imag = gam[0, rows, :], gam[1, rows, :]
        du = across[...] - line[:, 0:1]
        model_real = (line[:, 2:3] + line[:, 6:7] * dv) + line[:, 4:5] * du
        model_imag = (line[:, 3:4] + line[:, 7:8] * dv) + line[:, 5:6] * du
        ramped[0, inner, :] = real * model_real + imag * model_imag
        ramped[1, inner, :] = imag * model_real - real * model_imag
        coherence[inner, :] = jnp.sqrt(real * real + imag * imag)


def on_device(n_rows, n_cols, lead, trail, flags, sweep):
    height, width = flags.shape
    wide = width + LANES
    any_space = pl.BlockSpec(memory_space=pltpu.HBM)
    vmem = pl.BlockSpec(memory_space=pltpu.VMEM)
    dma = pltpu.SemaphoreType.DMA
    gam, coef, across = pl.pallas_call(
        functools.partial(front_kernel, n_rows, n_cols),
        out_shape=[
            pltpu.VMEM((2, height, width), F32),
            pltpu.VMEM((height, LANES), F32),
            pltpu.VMEM((8, width), F32),
        ],
        in_specs=[any_space, any_space, any_space, vmem],
        out_specs=[vmem, vmem, vmem],
        scratch_shapes=[
            pltpu.VMEM((2, height, width), F32),
            pltpu.VMEM((2, height, width), F32),
            pltpu.VMEM((height, width), jnp.int32),
            pltpu.VMEM((3, EDGE, width), F32),
            pltpu.VMEM((3, EDGE, width), F32),
            pltpu.VMEM((3, EDGE, width), F32),
            pltpu.VMEM((3, EDGE, width), F32),
            pltpu.VMEM((height, LANES), F32),
            pltpu.VMEM((height, LANES), F32),
            pltpu.VMEM((height, LANES), F32),
            pltpu.VMEM((height, LANES), F32),
            pltpu.VMEM((height, LANES), F32),
            pltpu.VMEM((EDGE, LANES), F32),
            pltpu.VMEM((EDGE, LANES), F32),
            pltpu.VMEM((4, 2 * height, wide), BF16),
            pltpu.VMEM((4, 4 * EDGE, wide), BF16),
            pltpu.VMEM((4, height, wide), F32),
            pltpu.VMEM((height, LANES), F32),
            pltpu.VMEM((LANES, height), F32),
            pltpu.VMEM((SWEEP_TALLY, LANES), F32),
            pltpu.VMEM((n_cols - 1, SWEEP_TALLY, LANES), F32),
            pltpu.VMEM((SWEEP_TALLY, LANES), F32),
            pltpu.VMEM((n_rows - 1, SWEEP_TALLY, LANES), F32),
            dma((3, 3)),
            dma((2,)), dma((2,)),
            dma((2,)), dma((2,)),
            dma((2,)), dma((2,)),
            dma((n_cols - 1,)), dma((n_cols - 1,)),
            dma((n_rows - 1,)), dma((n_rows - 1,)),
        ],
        compiler_params=pltpu.CompilerParams(
            collective_id=0, has_side_effects=True, vmem_limit_bytes=40 * 1024 * 1024
        ),
        name="front",
    )(lead, trail, flags, sweep.reshape(1, height))
    block = 32 if height % 32 == 0 else 8
    return pl.pallas_call(
        functools.partial(back_kernel, n_rows, block),
        grid=(height // block,),
        out_shape=[
            jax.ShapeDtypeStruct((2, height, width), F32),
            jax.ShapeDtypeStruct((height, width), F32),
        ],
        in_specs=[vmem, vmem, vmem],
        out_specs=[
            pl.BlockSpec((2, block, width), lambda r: (0, r, 0)),
            pl.BlockSpec((block, width), lambda r: (r, 0)),
        ],
        compiler_params=pltpu.CompilerParams(vmem_limit_bytes=16 * 1024 * 1024),
        name="back",
    )(gam, coef, across)


def solution(mesh):
    return jax.shard_map(
        functools.partial(on_device, mesh.shape["rows"], mesh.shape["cols"]),
        mesh=mesh,
        in_specs=(P(None, "rows", "cols"), P(None, "rows", "cols"), P("rows", "cols"), P("rows")),
        out_specs=(P(None, "rows", "cols"), P("rows", "cols")),
        check_vma=False,
    )
```

profile of v0, /device:TPU:0, one launch (start us, length us, event | category | flops | bytes accessed | tf_op | source)
XLA Modules:
  0.0 45.4 jit_solution(13210694401374942328)
XLA Ops:
  0.6 0.0 copy-start
  0.6 1.6 %copy-done = f32[2,128,2048]{2,1,0:T(8,128)S(1)} copy-done((f32[2,128,2048]{2,1,0:T(8,128)S(1)}, f32[2,128,2048]{2,1,0:T(8,128)}, u32[]{:S(2)}) %copy-start) | copy-done | bytes 2097176
  2.2 0.0 copy-start.1
  2.2 1.6 %copy-done.1 = f32[2,128,2048]{2,1,0:T(8,128)S(1)} copy-done((f32[2,128,2048]{2,1,0:T(8,128)S(1)}, f32[2,128,2048]{2,1,0:T(8,128)}, u32[]{:S(2)}) %copy-start.1) | copy-done | bytes 2097176
  3.8 0.0 copy-start.2
  3.8 1.2 %copy-done.2 = s32[128,2048]{1,0:T(8,128)S(1)} copy-done((s32[128,2048]{1,0:T(8,128)S(1)}, s32[128,2048]{1,0:T(8,128)}, u32[]{:S(2)}) %copy-start.2) | copy-done | bytes 1048600
  5.0 0.0 copy-start.3
  5.0 0.7 %copy-done.3 = s32[128]{0:T(128)S(1)} copy-done((s32[128]{0:T(128)S(1)}, s32[128]{0:T(128)}, u32[]{:S(2)}) %copy-start.3) | copy-done | bytes 536
  5.7 34.9 %front.1 = (f32[2,128,2048]{2,1,0:T(8,128)S(1)}, f32[128,128]{1,0:T(8,128)S(1)}, f32[8,2048]{1,0:T(8,128)S(1)}) custom-call(f32[2,128,2048]{2,1,0:T(8,128)S(1)} %copy-done, f32[2,128,2048]{2,1,0:T(8,128)S(1)} %copy-done.1, s32[128,2048]{1,0:T(8,128)S(1)} %copy-done.2, s32[1,128]{1,0:T(1,128)S(1)} %bitcast.1), custom_call_target="tpu_custom_call" | custom-call | tf_op jit(solution)/shard_map/front/pallas_call | solution.py:440
  40.7 4.8 %back.1 = (f32[2,128,2048]{2,1,0:T(8,128)}, f32[128,2048]{1,0:T(8,128)}) custom-call(f32[2,128,2048]{2,1,0:T(8,128)S(1)} %get-tuple-element.5.gam, f32[128,128]{1,0:T(8,128)S(1)} %get-tuple-element.6.coef, f32[8,2048]{1,0:T(8,128)S(1)} %get-tuple-element.7.across), custom_call_target="tpu_custom_call" | custom-call | tf_op jit(solution)/shard_map/back/pallas_call | solution.py:486
Async XLA Ops:
  0.6 1.6 %copy-start = (f32[2,128,2048]{2,1,0:T(8,128)S(1)}, f32[2,128,2048]{2,1,0:T(8,128)}, u32[]{:S(2)}) copy-start(f32[2,128,2048]{2,1,0:T(8,128)} %lead.1) | copy-start | bytes 6291460
  2.2 1.6 %copy-start.1 = (f32[2,128,2048]{2,1,0:T(8,128)S(1)}, f32[2,128,2048]{2,1,0:T(8,128)}, u32[]{:S(2)}) copy-start(f32[2,128,2048]{2,1,0:T(8,128)} %trail.1) | copy-start | bytes 6291460
  3.8 1.2 %copy-start.2 = (s32[128,2048]{1,0:T(8,128)S(1)}, s32[128,2048]{1,0:T(8,128)}, u32[]{:S(2)}) copy-start(s32[128,2048]{1,0:T(8,128)} %flags.1) | copy-start | bytes 3145732
  5.0 0.7 %copy-start.3 = (s32[128]{0:T(128)S(1)}, s32[128]{0:T(128)}, u32[]{:S(2)}) copy-start(s32[128]{0:T(128)} %param.7) | copy-start | bytes 1540
where the time goes:
time: 45.6 us; the launch traced here: 45.4 us
  Pallas kernels  39.7 us (87%)
  local copies, waits for them, and re-layouts  5.05 us (11%)
  between operations  0.65 us (1%)
    pallas_call x1, Pallas kernels, on_device(): pl.pallas_call(functools.partial(front_kernel, n_rows, n_cols), out_shape...  34.9 us
    unnamed x8, local copies, waits for them, and re-layouts  5.05 us
    pallas_call x1, Pallas kernels, on_device(): pl.pallas_call(functools.partial(back_kernel, n_rows, block), grid=(heigh...  4.76 us

commit v1 on v0

v1 whole, which is shorter than its diff:
```python
import functools

import jax
import jax.numpy as jnp
from jax import lax
from jax.experimental import pallas as pl
from jax.experimental.pallas import tpu as pltpu
from jax.sharding import PartitionSpec as P

WIN_R = 32
WIN_C = 8
SWEEP_TALLY = 16

EDGE = WIN_R // 2
SIDE = WIN_C // 2
LANES = 128
SCALE = 2.0**56
FLOOR = 1e-36
F32 = jnp.float32
BF16 = jnp.bfloat16
MESH = pl.DeviceIdType.MESH


def masked(av, bv, wv, rows, lanes):
    w = wv[rows, lanes].astype(F32)
    return av[0, rows, lanes] * w, av[1, rows, lanes] * w, bv[0, rows, lanes] * w, bv[1, rows, lanes] * w


def encode(ar, ai, br, bi):
    sr, si = ar * SCALE, ai * SCALE
    power = sr * sr + si * si
    some = power > FLOOR
    inverse = lax.rsqrt(jnp.where(some, power, 1.0))
    return (
        jnp.where(some, power * inverse * (1.0 / SCALE), 0.0),
        jnp.where(some, (sr * br + si * bi) * inverse, br),
        jnp.where(some, (si * br - sr * bi) * inverse, bi),
    )


def decode(s, gr, gi):
    return s * gr, s * gi, s * s, gr * gr + gi * gi


def put_split(out, products, lanes, rows, low_rows):
    for plane, value in enumerate(products):
        high = value.astype(BF16)
        low = (value - high.astype(F32)).astype(BF16)
        for where in lanes:
            out[plane, rows, where] = high
            out[plane, low_rows, where] = low


def edge_block(pack):
    lane = lax.broadcasted_iota(jnp.int32, pack.shape, 1)
    left, right = lane >= LANES - SIDE, lane < SIDE

    def pick(k):
        a = pack if k == 0 else pltpu.roll(pack, k * SIDE, 1)
        b = pack if k == 0 else pltpu.roll(pack, LANES - k * SIDE, 1)
        return jnp.where(left, a, jnp.where(right, b, 0.0))

    return pick(0), pick(1), pick(2)


def chunk_tiles(tiles):
    if tiles < 8:
        return ((0, tiles),)
    cuts = [0, tiles * 5 // 16, tiles * 10 // 16, tiles * 13 // 16, tiles]
    return tuple((a, b) for a, b in zip(cuts[:-1], cuts[1:]))


def fold(x):
    total = x[:, 0:LANES]
    for t in range(1, x.shape[1] // LANES):
        total = total + x[:, t * LANES : (t + 1) * LANES]
    return total


def front_kernel(
    n_rows, n_cols, reach,
    lead, trail, flags, sweep,
    gam, coh, memt, fit,
    av, bv, wv, sv, up_out, down_out, top_in, bot_in, left_out, right_out, left_in, right_in,
    corner, corner_top, corner_bot, split, halo_split, vert, across, edge_sums, acc_g, acc_h,
    tab_out, tab_in,
    load_sem, halo_send, halo_recv, side_send, side_recv, corner_send, corner_recv,
    tab_send, tab_recv,
):
    me_r, me_c = lax.axis_index("rows"), lax.axis_index("cols")
    height, width = flags.shape
    tiles = width // LANES
    low = height - EDGE
    total_rows, total_cols = height * n_rows, width * n_cols
    chunk = 512 if width % 512 == 0 else LANES
    has_up, has_down = me_r > 0, me_r < n_rows - 1
    has_left, has_right = me_c > 0, me_c < n_cols - 1
    pieces = chunk_tiles(tiles)
    early = max(1, len(pieces) // 2)

    def load(part, rows):
        group = [
            pltpu.make_async_copy(lead.at[:, rows, :], av.at[:, rows, :], load_sem.at[part, 0]),
            pltpu.make_async_copy(trail.at[:, rows, :], bv.at[:, rows, :], load_sem.at[part, 1]),
            pltpu.make_async_copy(flags.at[rows, :], wv.at[rows, :], load_sem.at[part, 2]),
        ]
        for copy in group:
            copy.start()
        return group

    loads = [load(0, pl.ds(low, EDGE)), load(1, pl.ds(0, EDGE)), load(2, pl.ds(EDGE, low - EDGE))]
    sweep_load = pltpu.make_async_copy(sweep, sv, load_sem.at[3, 0])
    sweep_load.start()

    barrier = pltpu.get_barrier_semaphore()
    peers = []
    for dr in range(-reach, reach + 1):
        for dc in range(n_cols):
            if dr == 0 and dc == 0:
                continue
            to = jnp.logical_and(me_r + dr >= 0, me_r + dr < n_rows)
            of = jnp.logical_and(me_r - dr >= 0, me_r - dr < n_rows)
            peers.append(((dr + reach) * n_cols + dc, to, of, me_r + dr, lax.rem(me_c + dc, n_cols)))
    for _, to, _, row, col in peers:
        @pl.when(to)
        def _():
            pl.semaphore_signal(barrier, inc=1, device_id=(row, col), device_id_type=MESH)

    n_peers = (jnp.minimum(me_r, reach) + jnp.minimum(n_rows - 1 - me_r, reach) + 1) * n_cols - 1

    def remote(src, dst, send, recv, row, col):
        return pltpu.make_async_remote_copy(
            src_ref=src, dst_ref=dst, send_sem=send, recv_sem=recv, device_id=(row, col), device_id_type=MESH
        )

    def cut(ref, piece):
        return ref.at[:, :, pl.ds(piece[0] * LANES, (piece[1] - piece[0]) * LANES)]

    downs = [
        remote(cut(down_out, p), cut(top_in, p), halo_send.at[0, i], halo_recv.at[0, i], me_r + 1, me_c)
        for i, p in enumerate(pieces)
    ]
    ups = [
        remote(cut(up_out, p), cut(bot_in, p), halo_send.at[1, i], halo_recv.at[1, i], me_r - 1, me_c)
        for i, p in enumerate(pieces)
    ]
    to_right = remote(right_out, left_in, side_send.at[0], side_recv.at[0], me_r, me_c + 1)
    to_left = remote(left_out, right_in, side_send.at[1], side_recv.at[1], me_r, me_c - 1)
    corner_down = remote(
        corner.at[pl.ds(low, EDGE)], corner_top, corner_send.at[0], corner_recv.at[0], me_r + 1, me_c
    )
    corner_up = remote(
        corner.at[pl.ds(0, EDGE)], corner_bot, corner_send.at[1], corner_recv.at[1], me_r - 1, me_c
    )

    def encode_rows(first, out, piece):
        lanes = pl.ds(piece[0] * LANES, (piece[1] - piece[0]) * LANES)
        for k, value in enumerate(encode(*masked(av, bv, wv, pl.ds(first, EDGE), lanes))):
            out[k, :, lanes] = value

    def send_piece(i):
        @pl.when(has_down)
        def _():
            downs[i].start()

        @pl.when(has_up)
        def _():
            ups[i].start()

    for copy in loads[0]:
        copy.wait()
    encode_rows(low, down_out, pieces[0])
    for copy in loads[1]:
        copy.wait()
    encode_rows(0, up_out, pieces[0])

    pl.semaphore_wait(barrier, n_peers)
    send_piece(0)
    for i in range(1, len(pieces)):
        encode_rows(low, down_out, pieces[i])
        encode_rows(0, up_out, pieces[i])
        if i < early:
            send_piece(i)

    for copy in loads[2]:
        copy.wait()

    @pl.loop(0, height // 16)
    def _(b):
        rows = pl.ds(pl.multiple_of(b * 16, 16), 16)
        lane = lax.broadcasted_iota(jnp.int32, (16, LANES), 1)
        s, gr, gi = encode(*masked(av, bv, wv, rows, pl.ds(width - LANES, LANES)))
        right_out[rows, :] = jnp.where(
            lane >= LANES - SIDE,
            s,
            jnp.where(
                lane >= LANES - 2 * SIDE,
                pltpu.roll(gr, LANES - SIDE, 1),
                jnp.where(lane >= LANES - 3 * SIDE, pltpu.roll(gi, LANES - 2 * SIDE, 1), 0.0),
            ),
        )
        s, gr, gi = encode(*masked(av, bv, wv, rows, pl.ds(0, LANES)))
        left_out[rows, :] = jnp.where(
            lane < SIDE,
            s,
            jnp.where(
                lane < 2 * SIDE,
                pltpu.roll(gr, SIDE, 1),
                jnp.where(lane < 3 * SIDE, pltpu.roll(gi, 2 * SIDE, 1), 0.0),
            ),
        )

    @pl.when(has_right)
    def _():
        to_right.start()

    @pl.when(has_left)
    def _():
        to_left.start()

    @pl.when(jnp.logical_not(has_left))
    def _():
        left_in[...] = jnp.zeros_like(left_in)

    @pl.when(jnp.logical_not(has_right))
    def _():
        right_in[...] = jnp.zeros_like(right_in)

    @pl.when(jnp.logical_not(has_up))
    def _():
        top_in[...] = jnp.zeros_like(top_in)
        corner_top[...] = jnp.zeros_like(corner_top)

    @pl.when(jnp.logical_not(has_down))
    def _():
        bot_in[...] = jnp.zeros_like(bot_in)
        corner_bot[...] = jnp.zeros_like(corner_bot)

    for slot, _, of, _, _ in peers:
        @pl.when(jnp.logical_not(of))
        def _():
            tab_in[slot] = jnp.zeros((1, 2 * LANES), F32)

    @pl.loop(0, height // 16)
    def _(b):
        rows = pl.ds(pl.multiple_of(b * 16, 16), 16)
        low_rows = pl.ds(pl.multiple_of(height + b * 16, 16), 16)

        @pl.loop(0, width // chunk)
        def _(c):
            lanes = pl.ds(pl.multiple_of(c * chunk, chunk), chunk)
            ar, ai, br, bi = masked(av, bv, wv, rows, lanes)
            put_split(
                split,
                (ar * br + ai * bi, ai * br - ar * bi, ar * ar + ai * ai, br * br + bi * bi),
                [pl.ds(pl.multiple_of(LANES + c * chunk, LANES), chunk)], rows, low_rows,
            )

    @pl.when(has_left)
    def _():
        to_right.wait_recv()

    @pl.when(has_right)
    def _():
        to_left.wait_recv()

    sides = [pl.ds(0, LANES), pl.ds(LANES + width, LANES)]

    @pl.loop(0, height // 16)
    def _(b):
        rows = pl.ds(pl.multiple_of(b * 16, 16), 16)
        low_rows = pl.ds(pl.multiple_of(height + b * 16, 16), 16)
        lane = lax.broadcasted_iota(jnp.int32, (16, LANES), 1)
        pack = jnp.where(lane >= LANES // 2, left_in[rows, :], right_in[rows, :])
        corner[rows, :] = pack
        put_split(split, decode(*edge_block(pack)), sides, rows, low_rows)

    @pl.when(has_down)
    def _():
        corner_down.start()

    @pl.when(has_up)
    def _():
        corner_up.start()

    for i in range(early, len(pieces)):
        send_piece(i)

    sweep_load.wait()
    lane_all = lax.broadcasted_iota(jnp.int32, (8, width), 1) + me_c * width
    across[...] = (lane_all.astype(F32) + 0.5) * (2.0 / total_cols) - 1.0
    kind = lax.rem(lax.broadcasted_iota(jnp.int32, (LANES, height), 0), SWEEP_TALLY)
    memt[...] = (kind == sv[...]).astype(F32).T
    acc_g[...] = jnp.zeros_like(acc_g)
    acc_h[...] = jnp.zeros_like(acc_h)
    edge_sums[...] = jnp.zeros_like(edge_sums)

    r = lax.broadcasted_iota(jnp.int32, (height, 2 * height), 0)
    k = lax.rem(lax.broadcasted_iota(jnp.int32, (height, 2 * height), 1), height)
    band = jnp.logical_and(k >= r - EDGE, k < r + EDGE).astype(F32).astype(BF16)
    span = 2 * LANES

    @pl.loop(0, (tiles + 2) // 2)
    def _(c):
        lanes = pl.ds(pl.multiple_of(c * span, span), span)
        for plane in range(4):
            vert[plane, :, lanes] = jnp.dot(band, split[plane, :, lanes], preferred_element_type=F32)

    group_lane = lax.broadcasted_iota(jnp.int32, (8, LANES), 1) // SWEEP_TALLY

    def row_v(first):
        row = lax.broadcasted_iota(jnp.int32, (8, LANES), 0) + (me_r * height + first)
        return (row.astype(F32) + 0.5) * (2.0 / total_rows) - 1.0

    def arrange(values):
        table = jnp.zeros((8, LANES), F32)
        for m, value in enumerate(values):
            table = jnp.where(group_lane == m, value, table)
        return table

    def row_sum(x):
        return jnp.sum(x, 1, keepdims=True)

    @pl.loop(0, height // 8)
    def _(b):
        first = pl.multiple_of(b * 8, 8)
        rows = pl.ds(first, 8)
        w = wv[rows, :].astype(F32)
        u = across[...]
        wu = w * u
        s0, su, suu = row_sum(fold(w)), row_sum(fold(wu)), row_sum(fold(wu * u))
        v = row_v(first)
        acc_g[...] += memt[rows, :] * arrange((s0, su, v * s0, suu, v * su, v * v * s0))

    def gamma(rows, t0, n):
        size = (n + 2) * LANES
        lanes = pl.ds(t0 * LANES, size)
        inner = pl.ds(t0 * LANES, n * LANES)

        def across_sum(plane):
            x = vert[plane, rows, lanes]
            x = x + pltpu.roll(x, size - 1, 1)
            x = x + pltpu.roll(x, size - 2, 1)
            return x + pltpu.roll(x, size - 4, 1)

        inverse = lax.rsqrt((across_sum(2) + 1.0) * (across_sum(3) + 1.0))
        real = pltpu.roll(across_sum(0) * inverse, SIDE, 1)[:, LANES : size - LANES]
        imag = pltpu.roll(across_sum(1) * inverse, SIDE, 1)[:, LANES : size - LANES]
        gam[0, rows, inner] = real
        gam[1, rows, inner] = imag
        coh[rows, inner] = jnp.sqrt(real * real + imag * imag)
        w = wv[rows, inner].astype(F32)
        wr, wi = w * real, w * imag
        u = across[:, inner]
        return fold(wr), fold(wi), fold(wr * u), fold(wi * u)

    def add_rows(first, sums):
        hr, hi, hur, hui = [row_sum(x) for x in sums]
        v = row_v(first)
        acc_h[...] += memt[pl.ds(first, 8), :] * arrange((hr, hi, hur, hui, v * hr, v * hi))

    half = tiles // 2 if tiles % 2 == 0 else tiles

    @pl.loop(0, (low - EDGE) // 8)
    def _(b):
        first = pl.multiple_of(EDGE + b * 8, 8)
        parts = [gamma(pl.ds(first, 8), t0, half) for t0 in range(0, tiles, half)]
        add_rows(first, [functools.reduce(jnp.add, x) for x in zip(*parts)])

    r = lax.broadcasted_iota(jnp.int32, (2 * EDGE, 4 * EDGE), 0)
    k = lax.broadcasted_iota(jnp.int32, (2 * EDGE, 4 * EDGE), 1)
    within = lax.rem(k, EDGE)
    upper = jnp.logical_and(jnp.logical_and(r < EDGE, k < 2 * EDGE), within >= r)
    lower = jnp.logical_and(jnp.logical_and(r >= EDGE, k >= 2 * EDGE), within < r - EDGE)
    reach_rows = jnp.logical_or(upper, lower).astype(F32).astype(BF16)

    def add_halo(sources, where):
        for part, products in enumerate(sources):
            put_split(
                halo_split, products, [where],
                pl.ds(2 * part * EDGE, EDGE), pl.ds((2 * part + 1) * EDGE, EDGE),
            )
        for plane in range(4):
            extra = jnp.dot(reach_rows, halo_split[plane, :, where], preferred_element_type=F32)
            vert[plane, 0:EDGE, where] += extra[:EDGE]
            vert[plane, low:height, where] += extra[EDGE:]

    def finish_edges(t0, n):
        @pl.loop(0, 2 * EDGE // 8)
        def _(b):
            first = pl.multiple_of(b * 8 + (b // (EDGE // 8)) * (low - EDGE), 8)
            for m, value in enumerate(gamma(pl.ds(first, 8), t0, n)):
                edge_sums[b, m] += value

    done = 1
    for i, piece in enumerate(pieces):
        if i == min(early, len(pieces) - 1):
            @pl.when(has_up)
            def _():
                corner_down.wait_recv()

            @pl.when(has_down)
            def _():
                corner_up.wait_recv()

            for where in sides:
                add_halo([decode(*edge_block(pack[...])) for pack in (corner_top, corner_bot)], where)

        @pl.when(has_up)
        def _():
            downs[i].wait_recv()

        @pl.when(has_down)
        def _():
            ups[i].wait_recv()

        source = pl.ds(piece[0] * LANES, (piece[1] - piece[0]) * LANES)
        target = pl.ds((piece[0] + 1) * LANES, (piece[1] - piece[0]) * LANES)
        add_halo([decode(*[halo[m, :, source] for m in range(3)]) for halo in (top_in, bot_in)], target)
        if i == min(early, len(pieces) - 1):
            finish_edges(0, 1)
        ready = tiles if i == len(pieces) - 1 else piece[1] - 1
        if ready > done:
            finish_edges(done, ready - done)
            done = ready

    for b in range(2 * EDGE // 8):
        first = b * 8 + (b // (EDGE // 8)) * (low - EDGE)
        add_rows(first, [edge_sums[b, m] for m in range(4)])

    tab_out[:, 0:LANES] = jnp.sum(acc_g[...], 0, keepdims=True)
    tab_out[:, LANES:] = jnp.sum(acc_h[...], 0, keepdims=True)
    swaps = [
        (remote(tab_out, tab_in.at[slot], tab_send.at[slot], tab_recv.at[slot], row, col), to, of)
        for slot, to, of, row, col in peers
    ]
    for copy, to, _ in swaps:
        @pl.when(to)
        def _():
            copy.start()

    tab_in[reach * n_cols] = tab_out[...]
    for copy, _, of in swaps:
        @pl.when(of)
        def _():
            copy.wait_recv()

    total = functools.reduce(jnp.add, [tab_in[slot] for slot in range(tab_in.shape[0])])

    def column(base, m):
        part = total[:, base : base + LANES]
        return part if m == 0 else pltpu.roll(part, LANES - m * SWEEP_TALLY, 1)

    s0, su, sv_, suu, suv, svv = [column(0, m) for m in range(6)]
    hr, hi, hur, hui, hvr, hvi = [column(LANES, m) for m in range(6)]
    floored = jnp.maximum(s0, 1.0)
    mid_u, mid_v = su / floored, sv_ / floored
    guu = suu - 2.0 * mid_u * su + mid_u * mid_u * s0
    guv = suv - mid_u * sv_ - mid_v * su + mid_u * mid_v * s0
    gvv = svv - 2.0 * mid_v * sv_ + mid_v * mid_v * s0
    hur, hui = hur - mid_u * hr, hui - mid_u * hi
    hvr, hvi = hvr - mid_v * hr, hvi - mid_v * hi
    ridge = 0.001 * s0 + 1.0
    duu, dvv = guu + ridge, gvv + ridge
    scale = 1.0 / (duu * dvv - guv * guv)
    base = 1.0 / (s0 + ridge)
    c1r, c1i = (dvv * hur - guv * hvr) * scale, (dvv * hui - guv * hvi) * scale
    c2r, c2i = (duu * hvr - guv * hur) * scale, (duu * hvi - guv * hui) * scale
    valid = lax.broadcasted_iota(jnp.int32, (1, LANES), 1) < SWEEP_TALLY
    rows_out = (hr * base - c1r * mid_u, hi * base - c1i * mid_u, c1r, c1i, c2r, c2i, mid_v)
    for m, value in enumerate(rows_out):
        fit[m : m + 1, :] = jnp.where(valid, value, 0.0)

    @pl.when(has_down)
    def _():
        for copy in downs:
            copy.wait_send()
        corner_down.wait_send()

    @pl.when(has_up)
    def _():
        for copy in ups:
            copy.wait_send()
        corner_up.wait_send()

    @pl.when(has_right)
    def _():
        to_right.wait_send()

    @pl.when(has_left)
    def _():
        to_left.wait_send()

    for copy, to, _ in swaps:
        @pl.when(to)
        def _():
            copy.wait_send()


def back_kernel(n_rows, n_cols, block, gam, coh, memt, fit, ramped, coherence, out, across, sem):
    height, width = coh.shape
    me_r, me_c = lax.axis_index("rows"), lax.axis_index("cols")
    coh_copy = pltpu.make_async_copy(coh, coherence, sem.at[0])
    coh_copy.start()
    lane_all = lax.broadcasted_iota(jnp.int32, (8, width), 1) + me_c * width
    across[...] = (lane_all.astype(F32) + 0.5) * (2.0 / (width * n_cols)) - 1.0

    def row_sum(x):
        return jnp.sum(x, 1, keepdims=True)

    copies = []
    for i in range(height // block):
        @pl.loop(0, block // 8)
        def _(b):
            first = pl.multiple_of(i * block + b * 8, 8)
            rows = pl.ds(first, 8)
            row = lax.broadcasted_iota(jnp.int32, (8, LANES), 0) + (me_r * height + first)
            v = (row.astype(F32) + 0.5) * (2.0 / (height * n_rows)) - 1.0
            one = memt[rows, :]
            dv = v - fit[6:7, :]
            base_r = row_sum(one * (fit[0:1, :] + fit[4:5, :] * dv))
            base_i = row_sum(one * (fit[1:2, :] + fit[5:6, :] * dv))
            slope_r = row_sum(one * fit[2:3, :])
            slope_i = row_sum(one * fit[3:4, :])
            real, imag = gam[0, rows, :], gam[1, rows, :]
            u = across[...]
            model_real = base_r + slope_r * u
            model_imag = base_i + slope_i * u
            out[0, rows, :] = real * model_real + imag * model_imag
            out[1, rows, :] = imag * model_real - real * model_imag

        rows = pl.ds(i * block, block)
        copy = pltpu.make_async_copy(out.at[:, rows, :], ramped.at[:, rows, :], sem.at[1 + i])
        copy.start()
        copies.append(copy)
    coh_copy.wait()
    for copy in copies:
        copy.wait()


def on_device(n_rows, n_cols, lead, trail, flags, sweep):
    height, width = flags.shape
    wide = width + 2 * LANES
    longest = 2 * height * n_rows // SWEEP_TALLY
    reach = max(1, min(n_rows - 1, (longest - 2) // height + 1))
    slots = (2 * reach + 1) * n_cols
    pieces = len(chunk_tiles(width // LANES))
    hbm = pl.BlockSpec(memory_space=pltpu.HBM)
    vmem = pl.BlockSpec(memory_space=pltpu.VMEM)
    dma = pltpu.SemaphoreType.DMA
    gam, coh, memt, fit = pl.pallas_call(
        functools.partial(front_kernel, n_rows, n_cols, reach),
        out_shape=[
            pltpu.VMEM((2, height, width), F32),
            pltpu.VMEM((height, width), F32),
            pltpu.VMEM((height, LANES), F32),
            pltpu.VMEM((8, LANES), F32),
        ],
        in_specs=[hbm, hbm, hbm, hbm],
        out_specs=[vmem, vmem, vmem, vmem],
        scratch_shapes=[
            pltpu.VMEM((2, height, width), F32),
            pltpu.VMEM((2, height, width), F32),
            pltpu.VMEM((height, width), jnp.int32),
            pltpu.VMEM((1, height), jnp.int32),
            pltpu.VMEM((3, EDGE, width), F32),
            pltpu.VMEM((3, EDGE, width), F32),
            pltpu.VMEM((3, EDGE, width), F32),
            pltpu.VMEM((3, EDGE, width), F32),
            pltpu.VMEM((height, LANES), F32),
            pltpu.VMEM((height, LANES), F32),
            pltpu.VMEM((height, LANES), F32),
            pltpu.VMEM((height, LANES), F32),
            pltpu.VMEM((height, LANES), F32),
            pltpu.VMEM((EDGE, LANES), F32),
            pltpu.VMEM((EDGE, LANES), F32),
            pltpu.VMEM((4, 2 * height, wide), BF16),
            pltpu.VMEM((4, 4 * EDGE, wide), BF16),
            pltpu.VMEM((4, height, wide), F32),
            pltpu.VMEM((8, width), F32),
            pltpu.VMEM((2 * EDGE // 8, 4, 8, LANES), F32),
            pltpu.VMEM((8, LANES), F32),
            pltpu.VMEM((8, LANES), F32),
            pltpu.VMEM((1, 2 * LANES), F32),
            pltpu.VMEM((slots, 1, 2 * LANES), F32),
            dma((4, 3)),
            dma((2, pieces)), dma((2, pieces)),
            dma((2,)), dma((2,)),
            dma((2,)), dma((2,)),
            dma((slots,)), dma((slots,)),
        ],
        compiler_params=pltpu.CompilerParams(
            collective_id=0, has_side_effects=True, vmem_limit_bytes=60 * 1024 * 1024
        ),
        name="front",
    )(lead, trail, flags, sweep.reshape(1, height))
    block = 16 if height % 16 == 0 else 8
    return pl.pallas_call(
        functools.partial(back_kernel, n_rows, n_cols, block),
        out_shape=[
            jax.ShapeDtypeStruct((2, height, width), F32),
            jax.ShapeDtypeStruct((height, width), F32),
        ],
        in_specs=[vmem, vmem, vmem, vmem],
        out_specs=[hbm, hbm],
        scratch_shapes=[
            pltpu.VMEM((2, height, width), F32),
            pltpu.VMEM((8, width), F32),
            dma((1 + height // block,)),
        ],
        compiler_params=pltpu.CompilerParams(vmem_limit_bytes=16 * 1024 * 1024),
        name="back",
    )(gam, coh, memt, fit)


def solution(mesh):
    return jax.shard_map(
        functools.partial(on_device, mesh.shape["rows"], mesh.shape["cols"]),
        mesh=mesh,
        in_specs=(P(None, "rows", "cols"), P(None, "rows", "cols"), P("rows", "cols"), P("rows")),
        out_specs=(P(None, "rows", "cols"), P("rows", "cols")),
        check_vma=False,
    )
```

time: 45.6 us -> 33.8 us (0.74)
  Pallas kernels: 39.7 us -> 33 us
  local copies, waits for them, and re-layouts: 5.05 us -> 0 us
    pallas_call x2, Pallas kernels: 39.7 us -> 33 us  [the longest x1 30.5 us: on_device(): pl.pallas_call(functools.partial(front_kernel, n_rows, n_cols, reach), ou...]
    unnamed x8 -> x0, local copies, waits for them, and re-layouts: 5.05 us -> none
where the time goes in v1:
time: 33.8 us; the launch traced here: 33.7 us
  Pallas kernels  33 us (98%)
  between operations  0.64 us (2%)
    pallas_call x1, Pallas kernels, on_device(): pl.pallas_call(functools.partial(front_kernel, n_rows, n_cols, reach), ou...  30.5 us
    pallas_call x1, Pallas kernels, on_device(): pl.pallas_call(functools.partial(back_kernel, n_rows, n_cols, block), out...  2.57 us

profile of v1, /device:TPU:0, one launch (start us, length us, event | category | flops | bytes accessed | tf_op | source)
XLA Modules:
  0.0 33.7 jit_solution(917602509342047403)
XLA Ops:
  0.6 30.5 %front.1 = (f32[2,128,2048]{2,1,0:T(8,128)S(1)}, f32[128,2048]{1,0:T(8,128)S(1)}, f32[128,128]{1,0:T(8,128)S(1)}, f32[8,128]{1,0:T(8,128)S(1)}) custom-call(f32[2,128,2048]{2,1,0:T(8,128)} %lead.1, f32[2,128,2048]{2,1,0:T(8,128)} %trail.1, s32[128,2048]{1,0:T(8,128)} %flags.1, s32[1,128]{1,0:T(1,128)} %bitcast.1), custom_call_target="tpu_custom_call" | custom-call | tf_op jit(solution)/shard_map/front/pallas_call | solution.py:551
  31.1 2.6 %back.1 = (f32[2,128,2048]{2,1,0:T(8,128)}, f32[128,2048]{1,0:T(8,128)}) custom-call(f32[2,128,2048]{2,1,0:T(8,128)S(1)} %get-tuple-element.6.gam, f32[128,2048]{1,0:T(8,128)S(1)} %get-tuple-element.7.coh, f32[128,128]{1,0:T(8,128)S(1)} %get-tuple-element.8.memt, f32[8,128]{1,0:T(8,128)S(1)} %get-tuple-element.9.fit), custom_call_target="tpu_custom_call" | custom-call | tf_op jit(solution)/shard_map/back/pallas_call | solution.py:598

commit v2 on v1

--- a/solution.py
+++ b/solution.py
@@ -42,13 +42,13 @@
     return s * gr, s * gi, s * s, gr * gr + gi * gi
 
 
-def put_split(out, products, lanes, rows, low_rows):
+def put_split(out, products, places):
     for plane, value in enumerate(products):
         high = value.astype(BF16)
         low = (value - high.astype(F32)).astype(BF16)
-        for where in lanes:
-            out[plane, rows, where] = high
-            out[plane, low_rows, where] = low
+        for rows, lanes in places:
+            out[0, plane, rows, lanes] = high
+            out[1, plane, rows, lanes] = low
 
 
 def edge_block(pack):
@@ -63,11 +63,11 @@
     return pick(0), pick(1), pick(2)
 
 
-def chunk_tiles(tiles):
+def cuts(tiles):
     if tiles < 8:
         return ((0, tiles),)
-    cuts = [0, tiles * 5 // 16, tiles * 10 // 16, tiles * 13 // 16, tiles]
-    return tuple((a, b) for a, b in zip(cuts[:-1], cuts[1:]))
+    marks = [0, tiles // 4, tiles // 2, tiles * 3 // 4, tiles - 1, tiles]
+    return tuple(zip(marks[:-1], marks[1:]))
 
 
 def fold(x):
@@ -77,12 +77,16 @@
     return total
 
 
+def row_sum(x):
+    return jnp.sum(x, 1, keepdims=True)
+
+
 def front_kernel(
     n_rows, n_cols, reach,
     lead, trail, flags, sweep,
     gam, coh, memt, fit,
     av, bv, wv, sv, up_out, down_out, top_in, bot_in, left_out, right_out, left_in, right_in,
-    corner, corner_top, corner_bot, split, halo_split, vert, across, edge_sums, acc_g, acc_h,
+    corner, corner_top, corner_bot, split, halo_split, boxed, ribbon, across, row_parts, flag_parts, acc_h,
     tab_out, tab_in,
     load_sem, halo_send, halo_recv, side_send, side_recv, corner_send, corner_recv,
     tab_send, tab_recv,
@@ -95,8 +99,9 @@
     chunk = 512 if width % 512 == 0 else LANES
     has_up, has_down = me_r > 0, me_r < n_rows - 1
     has_left, has_right = me_c > 0, me_c < n_cols - 1
-    pieces = chunk_tiles(tiles)
+    pieces = cuts(tiles)
     early = max(1, len(pieces) // 2)
+    pair = 2 if tiles % 2 == 0 else 1
 
     def load(part, rows):
         group = [
@@ -185,9 +190,8 @@
     for copy in loads[2]:
         copy.wait()
 
-    @pl.loop(0, height // 16)
-    def _(b):
-        rows = pl.ds(pl.multiple_of(b * 16, 16), 16)
+    for b in range(height // 16):
+        rows = pl.ds(b * 16, 16)
         lane = lax.broadcasted_iota(jnp.int32, (16, LANES), 1)
         s, gr, gi = encode(*masked(av, bv, wv, rows, pl.ds(width - LANES, LANES)))
         right_out[rows, :] = jnp.where(
@@ -241,10 +245,12 @@
         def _():
             tab_in[slot] = jnp.zeros((1, 2 * LANES), F32)
 
+    lane_all = lax.broadcasted_iota(jnp.int32, (8, width), 1) + me_c * width
+    across[...] = (lane_all.astype(F32) + 0.5) * (2.0 / total_cols) - 1.0
+
     @pl.loop(0, height // 16)
     def _(b):
         rows = pl.ds(pl.multiple_of(b * 16, 16), 16)
-        low_rows = pl.ds(pl.multiple_of(height + b * 16, 16), 16)
 
         @pl.loop(0, width // chunk)
         def _(c):
@@ -253,9 +259,29 @@
             put_split(
                 split,
                 (ar * br + ai * bi, ai * br - ar * bi, ar * ar + ai * ai, br * br + bi * bi),
-                [pl.ds(pl.multiple_of(LANES + c * chunk, LANES), chunk)], rows, low_rows,
+                [(rows, pl.ds(pl.multiple_of(LANES + c * chunk, LANES), chunk))],
             )
 
+    reach_in = (pair + 2) * LANES
+    i = lax.broadcasted_iota(jnp.int32, (reach_in, pair * LANES), 0)
+    j = lax.broadcasted_iota(jnp.int32, (reach_in, pair * LANES), 1) + LANES
+    ribbon[...] = jnp.logical_and(i >= j - SIDE, i < j + SIDE).astype(F32).astype(BF16)
+
+    def box_across(source, j, targets):
+        inner = pl.ds(pl.multiple_of(j * pair * LANES, pair * LANES), reach_in)
+        outer = pl.ds(pl.multiple_of(j * pair * LANES, pair * LANES), pair * LANES)
+        for plane in range(4):
+            sums = jnp.dot(source[0, plane, :, inner], ribbon[...], preferred_element_type=F32)
+            sums = sums + jnp.dot(source[1, plane, :, inner], ribbon[...], preferred_element_type=F32)
+            for first, target, count in targets:
+                boxed[plane, target : target + count, outer] = sums[first : first + count]
+
+    own = [(0, EDGE, height)]
+
+    @pl.loop(1, max(1, tiles // pair - 1))
+    def _(j):
+        box_across(split, j, own)
+
     @pl.when(has_left)
     def _():
         to_right.wait_recv()
@@ -265,15 +291,12 @@
         to_left.wait_recv()
 
     sides = [pl.ds(0, LANES), pl.ds(LANES + width, LANES)]
-
-    @pl.loop(0, height // 16)
-    def _(b):
-        rows = pl.ds(pl.multiple_of(b * 16, 16), 16)
-        low_rows = pl.ds(pl.multiple_of(height + b * 16, 16), 16)
+    for b in range(height // 16):
+        rows = pl.ds(b * 16, 16)
         lane = lax.broadcasted_iota(jnp.int32, (16, LANES), 1)
         pack = jnp.where(lane >= LANES // 2, left_in[rows, :], right_in[rows, :])
         corner[rows, :] = pack
-        put_split(split, decode(*edge_block(pack)), sides, rows, low_rows)
+        put_split(split, decode(*edge_block(pack)), [(rows, lanes) for lanes in sides])
 
     @pl.when(has_down)
     def _():
@@ -286,115 +309,108 @@
     for i in range(early, len(pieces)):
         send_piece(i)
 
+    for j in sorted({0, tiles // pair - 1}):
+        box_across(split, j, own)
+
     sweep_load.wait()
-    lane_all = lax.broadcasted_iota(jnp.int32, (8, width), 1) + me_c * width
-    across[...] = (lane_all.astype(F32) + 0.5) * (2.0 / total_cols) - 1.0
     kind = lax.rem(lax.broadcasted_iota(jnp.int32, (LANES, height), 0), SWEEP_TALLY)
     memt[...] = (kind == sv[...]).astype(F32).T
-    acc_g[...] = jnp.zeros_like(acc_g)
-    acc_h[...] = jnp.zeros_like(acc_h)
-    edge_sums[...] = jnp.zeros_like(edge_sums)
-
-    r = lax.broadcasted_iota(jnp.int32, (height, 2 * height), 0)
-    k = lax.rem(lax.broadcasted_iota(jnp.int32, (height, 2 * height), 1), height)
-    band = jnp.logical_and(k >= r - EDGE, k < r + EDGE).astype(F32).astype(BF16)
-    span = 2 * LANES
-
-    @pl.loop(0, (tiles + 2) // 2)
-    def _(c):
-        lanes = pl.ds(pl.multiple_of(c * span, span), span)
-        for plane in range(4):
-            vert[plane, :, lanes] = jnp.dot(band, split[plane, :, lanes], preferred_element_type=F32)
+    row_parts[...] = jnp.zeros_like(row_parts)
 
     group_lane = lax.broadcasted_iota(jnp.int32, (8, LANES), 1) // SWEEP_TALLY
 
-    def row_v(first):
-        row = lax.broadcasted_iota(jnp.int32, (8, LANES), 0) + (me_r * height + first)
+    def row_v(group):
+        row = lax.broadcasted_iota(jnp.int32, (8, LANES), 0) + (me_r * height + group * 8)
         return (row.astype(F32) + 0.5) * (2.0 / total_rows) - 1.0
 
-    def arrange(values):
-        table = jnp.zeros((8, LANES), F32)
+    def arrange(group, values):
+        table = values[0]
         for m, value in enumerate(values):
-            table = jnp.where(group_lane == m, value, table)
-        return table
-
-    def row_sum(x):
-        return jnp.sum(x, 1, keepdims=True)
+            table = value if m == 0 else jnp.where(group_lane >= m, value, table)
+        return memt[group * 8 : group * 8 + 8, :] * jnp.where(group_lane < len(values), table, 0.0)
 
     @pl.loop(0, height // 8)
     def _(b):
-        first = pl.multiple_of(b * 8, 8)
-        rows = pl.ds(first, 8)
-        w = wv[rows, :].astype(F32)
+        w = wv[pl.ds(pl.multiple_of(b * 8, 8), 8), :].astype(F32)
         u = across[...]
         wu = w * u
-        s0, su, suu = row_sum(fold(w)), row_sum(fold(wu)), row_sum(fold(wu * u))
-        v = row_v(first)
-        acc_g[...] += memt[rows, :] * arrange((s0, su, v * s0, suu, v * su, v * v * s0))
-
-    def gamma(rows, t0, n):
-        size = (n + 2) * LANES
-        lanes = pl.ds(t0 * LANES, size)
-        inner = pl.ds(t0 * LANES, n * LANES)
-
-        def across_sum(plane):
-            x = vert[plane, rows, lanes]
-            x = x + pltpu.roll(x, size - 1, 1)
-            x = x + pltpu.roll(x, size - 2, 1)
-            return x + pltpu.roll(x, size - 4, 1)
-
-        inverse = lax.rsqrt((across_sum(2) + 1.0) * (across_sum(3) + 1.0))
-        real = pltpu.roll(across_sum(0) * inverse, SIDE, 1)[:, LANES : size - LANES]
-        imag = pltpu.roll(across_sum(1) * inverse, SIDE, 1)[:, LANES : size - LANES]
-        gam[0, rows, inner] = real
-        gam[1, rows, inner] = imag
-        coh[rows, inner] = jnp.sqrt(real * real + imag * imag)
-        w = wv[rows, inner].astype(F32)
-        wr, wi = w * real, w * imag
-        u = across[:, inner]
-        return fold(wr), fold(wi), fold(wr * u), fold(wi * u)
-
-    def add_rows(first, sums):
-        hr, hi, hur, hui = [row_sum(x) for x in sums]
-        v = row_v(first)
-        acc_h[...] += memt[pl.ds(first, 8), :] * arrange((hr, hi, hur, hui, v * hr, v * hi))
-
-    half = tiles // 2 if tiles % 2 == 0 else tiles
-
-    @pl.loop(0, (low - EDGE) // 8)
-    def _(b):
-        first = pl.multiple_of(EDGE + b * 8, 8)
-        parts = [gamma(pl.ds(first, 8), t0, half) for t0 in range(0, tiles, half)]
-        add_rows(first, [functools.reduce(jnp.add, x) for x in zip(*parts)])
-
-    r = lax.broadcasted_iota(jnp.int32, (2 * EDGE, 4 * EDGE), 0)
-    k = lax.broadcasted_iota(jnp.int32, (2 * EDGE, 4 * EDGE), 1)
-    within = lax.rem(k, EDGE)
-    upper = jnp.logical_and(jnp.logical_and(r < EDGE, k < 2 * EDGE), within >= r)
-    lower = jnp.logical_and(jnp.logical_and(r >= EDGE, k >= 2 * EDGE), within < r - EDGE)
-    reach_rows = jnp.logical_or(upper, lower).astype(F32).astype(BF16)
-
-    def add_halo(sources, where):
+        for m, value in enumerate((w, wu, wu * u)):
+            flag_parts[b, m] = fold(value)
+
+    acc_g = None
+    for b in range(height // 8):
+        s0, su, suu = [row_sum(flag_parts[b, m]) for m in range(3)]
+        v = row_v(b)
+        part = arrange(b, (s0, su, v * s0, suu, v * su, v * v * s0))
+        acc_g = part if acc_g is None else acc_g + part
+    tab_out[:, 0:LANES] = jnp.sum(acc_g, 0, keepdims=True)
+
+    sub = lax.broadcasted_iota(jnp.int32, (8, LANES), 0)
+
+    def finish(t, top, bottom):
+        lanes = pl.ds(pl.multiple_of(t * LANES, LANES), LANES)
+        u = across[:, lanes]
+        state = [None] * 4
+        for g in range(bottom + 3, top - 1, -1):
+            window = []
+            for plane in range(4):
+                x = boxed[plane, g * 8 : g * 8 + 8, lanes]
+                r1 = pltpu.roll(x, 7, 0)
+                if state[plane] is None:
+                    state[plane] = (r1, None, None, None, None, None)
+                    y1 = x + r1
+                    r2 = pltpu.roll(y1, 6, 0)
+                    y2 = y1 + r2
+                    r4 = pltpu.roll(y2, 4, 0)
+                    state[plane] = (r1, r2, r4, None, None, None)
+                    continue
+                n1, n2, n4, last, pair1, pair2 = state[plane]
+                y1 = x + jnp.where(sub < 7, r1, n1)
+                r2 = pltpu.roll(y1, 6, 0)
+                y2 = y1 + jnp.where(sub < 6, r2, n2)
+                r4 = pltpu.roll(y2, 4, 0)
+                y4 = y2 + jnp.where(sub < 4, r4, n4)
+                both = None if last is None else y4 + last
+                window.append(None if pair2 is None else both + pair2)
+                state[plane] = (r1, r2, r4, y4, both, pair1)
+            if len(window) < 4 or window[0] is None:
+                continue
+            rows = slice(g * 8, g * 8 + 8)
+            inverse = lax.rsqrt((window[2] + 1.0) * (window[3] + 1.0))
+            real, imag = window[0] * inverse, window[1] * inverse
+            gam[0, rows, lanes] = real
+            gam[1, rows, lanes] = imag
+            coh[rows, lanes] = jnp.sqrt(real * real + imag * imag)
+            w = wv[rows, lanes].astype(F32)
+            wr, wi = w * real, w * imag
+            for m, value in enumerate((wr, wi, wr * u, wi * u)):
+                row_parts[g, m] += value
+
+    def add_rows(groups):
+        total = None
+        for g in groups:
+            hr, hi, hur, hui = [row_sum(row_parts[g, m]) for m in range(4)]
+            v = row_v(g)
+            part = arrange(g, (hr, hi, hur, hui, v * hr, v * hi))
+            total = part if total is None else total + part
+        return total
+
+    edge_groups, groups = EDGE // 8, height // 8
+
+    @pl.loop(0, tiles)
+    def _(t):
+        finish(t, edge_groups, groups - edge_groups)
+
+    acc_h[...] = add_rows(range(edge_groups, groups - edge_groups))
+
+    def put_halo(sources, where):
         for part, products in enumerate(sources):
-            put_split(
-                halo_split, products, [where],
-                pl.ds(2 * part * EDGE, EDGE), pl.ds((2 * part + 1) * EDGE, EDGE),
-            )
-        for plane in range(4):
-            extra = jnp.dot(reach_rows, halo_split[plane, :, where], preferred_element_type=F32)
-            vert[plane, 0:EDGE, where] += extra[:EDGE]
-            vert[plane, low:height, where] += extra[EDGE:]
-
-    def finish_edges(t0, n):
-        @pl.loop(0, 2 * EDGE // 8)
-        def _(b):
-            first = pl.multiple_of(b * 8 + (b // (EDGE // 8)) * (low - EDGE), 8)
-            for m, value in enumerate(gamma(pl.ds(first, 8), t0, n)):
-                edge_sums[b, m] += value
-
-    done = 1
+            put_split(halo_split, products, [(pl.ds(part * EDGE, EDGE), lanes) for lanes in where])
+
+    beyond = [(0, 0, EDGE), (EDGE, EDGE + height, EDGE)]
+    done = 0
     for i, piece in enumerate(pieces):
-        if i == min(early, len(pieces) - 1):
+        if i == 0:
             @pl.when(has_up)
             def _():
                 corner_down.wait_recv()
@@ -403,8 +419,7 @@
             def _():
                 corner_up.wait_recv()
 
-            for where in sides:
-                add_halo([decode(*edge_block(pack[...])) for pack in (corner_top, corner_bot)], where)
+            put_halo([decode(*edge_block(pack[...])) for pack in (corner_top, corner_bot)], sides)
 
         @pl.when(has_up)
         def _():
@@ -416,20 +431,19 @@
 
         source = pl.ds(piece[0] * LANES, (piece[1] - piece[0]) * LANES)
         target = pl.ds((piece[0] + 1) * LANES, (piece[1] - piece[0]) * LANES)
-        add_halo([decode(*[halo[m, :, source] for m in range(3)]) for halo in (top_in, bot_in)], target)
-        if i == min(early, len(pieces) - 1):
-            finish_edges(0, 1)
-        ready = tiles if i == len(pieces) - 1 else piece[1] - 1
+        put_halo([decode(*[halo[m, :, source] for m in range(3)]) for halo in (top_in, bot_in)], [target])
+        ready = tiles // pair if i == len(pieces) - 1 else max(0, (piece[1] - 1) // pair)
+        for j in range(done, ready):
+            box_across(halo_split, j, beyond)
         if ready > done:
-            finish_edges(done, ready - done)
-            done = ready
-
-    for b in range(2 * EDGE // 8):
-        first = b * 8 + (b // (EDGE // 8)) * (low - EDGE)
-        add_rows(first, [edge_sums[b, m] for m in range(4)])
-
-    tab_out[:, 0:LANES] = jnp.sum(acc_g[...], 0, keepdims=True)
-    tab_out[:, LANES:] = jnp.sum(acc_h[...], 0, keepdims=True)
+            @pl.loop(done * pair, ready * pair)
+            def _(t):
+                finish(t, 0, edge_groups)
+                finish(t, groups - edge_groups, groups)
+        done = ready
+
+    acc_last = acc_h[...] + add_rows(list(range(edge_groups)) + list(range(groups - edge_groups, groups)))
+    tab_out[:, LANES:] = jnp.sum(acc_last, 0, keepdims=True)
     swaps = [
         (remote(tab_out, tab_in.at[slot], tab_send.at[slot], tab_recv.at[slot], row, col), to, of)
         for slot, to, of, row, col in peers
@@ -504,9 +518,6 @@
     coh_copy.start()
     lane_all = lax.broadcasted_iota(jnp.int32, (8, width), 1) + me_c * width
     across[...] = (lane_all.astype(F32) + 0.5) * (2.0 / (width * n_cols)) - 1.0
-
-    def row_sum(x):
-        return jnp.sum(x, 1, keepdims=True)
 
     copies = []
     for i in range(height // block):
@@ -544,7 +555,8 @@
     longest = 2 * height * n_rows // SWEEP_TALLY
     reach = max(1, min(n_rows - 1, (longest - 2) // height + 1))
     slots = (2 * reach + 1) * n_cols
-    pieces = len(chunk_tiles(width // LANES))
+    pieces = len(cuts(width // LANES))
+    pair = 2 if width // LANES % 2 == 0 else 1
     hbm = pl.BlockSpec(memory_space=pltpu.HBM)
     vmem = pl.BlockSpec(memory_space=pltpu.VMEM)
     dma = pltpu.SemaphoreType.DMA
@@ -574,12 +586,13 @@
             pltpu.VMEM((height, LANES), F32),
             pltpu.VMEM((EDGE, LANES), F32),
             pltpu.VMEM((EDGE, LANES), F32),
-            pltpu.VMEM((4, 2 * height, wide), BF16),
-            pltpu.VMEM((4, 4 * EDGE, wide), BF16),
-            pltpu.VMEM((4, height, wide), F32),
+            pltpu.VMEM((2, 4, height, wide), BF16),
+            pltpu.VMEM((2, 4, 2 * EDGE, wide), BF16),
+            pltpu.VMEM((4, height + 2 * EDGE, width), F32),
+            pltpu.VMEM(((pair + 2) * LANES, pair * LANES), BF16),
             pltpu.VMEM((8, width), F32),
-            pltpu.VMEM((2 * EDGE // 8, 4, 8, LANES), F32),
-            pltpu.VMEM((8, LANES), F32),
+            pltpu.VMEM((height // 8, 4, 8, LANES), F32),
+            pltpu.VMEM((height // 8, 3, 8, LANES), F32),
             pltpu.VMEM((8, LANES), F32),
             pltpu.VMEM((1, 2 * LANES), F32),
             pltpu.VMEM((slots, 1, 2 * LANES), F32),

time: 33.8 us -> 31.5 us (0.932)
  Pallas kernels: 33 us -> 30.7 us
    pallas_call x1, Pallas kernels: 30.5 us -> 28.2 us  [on_device(): pl.pallas_call(functools.partial(front_kernel, n_rows, n_cols, reach), ou...]
where the time goes in v2:
time: 31.5 us; the launch traced here: 31.4 us
  Pallas kernels  30.7 us (97%)
  between operations  0.64 us (2%)
    pallas_call x1, Pallas kernels, on_device(): pl.pallas_call(functools.partial(front_kernel, n_rows, n_cols, reach), ou...  28.2 us
    pallas_call x1, Pallas kernels, on_device(): pl.pallas_call(functools.partial(back_kernel, n_rows, n_cols, block), out...  2.57 us

profile of v2, /device:TPU:0, one launch (start us, length us, event | category | flops | bytes accessed | tf_op | source)
XLA Modules:
  0.0 31.4 jit_solution(10056752614598428732)
XLA Ops:
  0.6 28.2 %front.1 = (f32[2,128,2048]{2,1,0:T(8,128)S(1)}, f32[128,2048]{1,0:T(8,128)S(1)}, f32[128,128]{1,0:T(8,128)S(1)}, f32[8,128]{1,0:T(8,128)S(1)}) custom-call(f32[2,128,2048]{2,1,0:T(8,128)} %lead.1, f32[2,128,2048]{2,1,0:T(8,128)} %trail.1, s32[128,2048]{1,0:T(8,128)} %flags.1, s32[1,128]{1,0:T(1,128)} %bitcast.1), custom_call_target="tpu_custom_call" | custom-call | tf_op jit(solution)/shard_map/front/pallas_call | solution.py:563
  28.8 2.6 %back.1 = (f32[2,128,2048]{2,1,0:T(8,128)}, f32[128,2048]{1,0:T(8,128)}) custom-call(f32[2,128,2048]{2,1,0:T(8,128)S(1)} %get-tuple-element.6.gam, f32[128,2048]{1,0:T(8,128)S(1)} %get-tuple-element.7.coh, f32[128,128]{1,0:T(8,128)S(1)} %get-tuple-element.8.memt, f32[8,128]{1,0:T(8,128)S(1)} %get-tuple-element.9.fit), custom_call_target="tpu_custom_call" | custom-call | tf_op jit(solution)/shard_map/back/pallas_call | solution.py:611

commit v3 on v2

--- a/solution.py
+++ b/solution.py
@@ -86,10 +86,10 @@
     lead, trail, flags, sweep,
     gam, coh, memt, fit,
     av, bv, wv, sv, up_out, down_out, top_in, bot_in, left_out, right_out, left_in, right_in,
-    corner, corner_top, corner_bot, split, halo_split, boxed, ribbon, across, row_parts, flag_parts, acc_h,
+    relay_in, corner_in, split, halo_split, boxed, ribbon, across, row_parts, flag_parts, acc_h,
     tab_out, tab_in,
     load_sem, halo_send, halo_recv, side_send, side_recv, corner_send, corner_recv,
-    tab_send, tab_recv,
+    relay_send, relay_recv, tab_send, tab_recv,
 ):
     me_r, me_c = lax.axis_index("rows"), lax.axis_index("cols")
     height, width = flags.shape
@@ -100,7 +100,6 @@
     has_up, has_down = me_r > 0, me_r < n_rows - 1
     has_left, has_right = me_c > 0, me_c < n_cols - 1
     pieces = cuts(tiles)
-    early = max(1, len(pieces) // 2)
     pair = 2 if tiles % 2 == 0 else 1
 
     def load(part, rows):
@@ -151,46 +150,50 @@
     ]
     to_right = remote(right_out, left_in, side_send.at[0], side_recv.at[0], me_r, me_c + 1)
     to_left = remote(left_out, right_in, side_send.at[1], side_recv.at[1], me_r, me_c - 1)
-    corner_down = remote(
-        corner.at[pl.ds(low, EDGE)], corner_top, corner_send.at[0], corner_recv.at[0], me_r + 1, me_c
-    )
-    corner_up = remote(
-        corner.at[pl.ds(0, EDGE)], corner_bot, corner_send.at[1], corner_recv.at[1], me_r - 1, me_c
-    )
+    top_rows, low_rows = pl.ds(0, EDGE), pl.ds(low, EDGE)
+    corners = []
+    for k, (src, rows, dr, dc, to, of) in enumerate((
+        (right_out, low_rows, 1, 1, has_down & has_right, has_up & has_left),
+        (left_out, low_rows, 1, -1, has_down & has_left, has_up & has_right),
+        (right_out, top_rows, -1, 1, has_up & has_right, has_down & has_left),
+        (left_out, top_rows, -1, -1, has_up & has_left, has_down & has_right),
+    )):
+        copy = remote(src.at[rows], corner_in.at[k], corner_send.at[k], corner_recv.at[k], me_r + dr, me_c + dc)
+        corners.append((copy, to, of))
+
+    relayed = len(pieces) - 2 if n_rows % 2 == 0 and n_rows > 2 and len(pieces) > 2 else 0
+    odd = lax.rem(me_r, 2) == 1
+    even = jnp.logical_not(odd)
+    place = lax.div(me_r, 2) * 4
+    n_up = jnp.minimum(relayed, lax.div(place, n_rows // 2)) if relayed else 0
+    n_down = jnp.minimum(relayed, 4 - lax.div(place + 4, n_rows // 2)) if relayed else 0
+    via = []
+    for i in range(relayed):
+        p = pieces[i]
+        ask_up, ask_down = even & (n_up > i), odd & (n_down > i)
+        give_up, give_down = odd & (n_up > i), even & (n_down > i)
+        via.append((
+            (ask_up, remote(cut(up_out, p), cut(relay_in, p), halo_send.at[1, i], relay_recv.at[i], me_r + 1, me_c)),
+            (ask_down, remote(cut(down_out, p), cut(relay_in, p), halo_send.at[0, i], relay_recv.at[i], me_r - 1, me_c)),
+            (give_up, remote(cut(relay_in, p), cut(bot_in, p), relay_send.at[i], halo_recv.at[1, i], me_r - 2, me_c)),
+            (give_down, remote(cut(relay_in, p), cut(top_in, p), relay_send.at[i], halo_recv.at[0, i], me_r + 2, me_c)),
+        ))
+
+    def forward(i):
+        if i >= relayed:
+            return
+        for give, copy in via[i][2:]:
+            @pl.when(give)
+            def _():
+                via[i][0][1].wait_recv()
+                copy.start()
 
     def encode_rows(first, out, piece):
         lanes = pl.ds(piece[0] * LANES, (piece[1] - piece[0]) * LANES)
         for k, value in enumerate(encode(*masked(av, bv, wv, pl.ds(first, EDGE), lanes))):
             out[k, :, lanes] = value
 
-    def send_piece(i):
-        @pl.when(has_down)
-        def _():
-            downs[i].start()
-
-        @pl.when(has_up)
-        def _():
-            ups[i].start()
-
-    for copy in loads[0]:
-        copy.wait()
-    encode_rows(low, down_out, pieces[0])
-    for copy in loads[1]:
-        copy.wait()
-    encode_rows(0, up_out, pieces[0])
-
-    pl.semaphore_wait(barrier, n_peers)
-    send_piece(0)
-    for i in range(1, len(pieces)):
-        encode_rows(low, down_out, pieces[i])
-        encode_rows(0, up_out, pieces[i])
-        if i < early:
-            send_piece(i)
-
-    for copy in loads[2]:
-        copy.wait()
-
-    for b in range(height // 16):
+    def pack_sides(b):
         rows = pl.ds(b * 16, 16)
         lane = lax.broadcasted_iota(jnp.int32, (16, LANES), 1)
         s, gr, gi = encode(*masked(av, bv, wv, rows, pl.ds(width - LANES, LANES)))
@@ -214,6 +217,46 @@
             ),
         )
 
+    for copy in loads[0] + loads[1]:
+        copy.wait()
+    for b in (0, height // 16 - 1):
+        pack_sides(b)
+    for piece in pieces:
+        encode_rows(low, down_out, piece)
+        encode_rows(0, up_out, piece)
+
+    pl.semaphore_wait(barrier, n_peers)
+    for copy, to, _ in corners:
+        @pl.when(to)
+        def _():
+            copy.start()
+
+    for group in via:
+        for ask, copy in group[:2]:
+            @pl.when(ask)
+            def _():
+                copy.start()
+
+    for i in range(len(pieces)):
+        straight_down, straight_up = has_down, has_up
+        if i < relayed:
+            straight_down &= jnp.logical_not(via[i][1][0])
+            straight_up &= jnp.logical_not(via[i][0][0])
+
+        @pl.when(straight_down)
+        def _():
+            downs[i].start()
+
+        @pl.when(straight_up)
+        def _():
+            ups[i].start()
+
+    for copy in loads[2]:
+        copy.wait()
+
+    for b in range(1, height // 16 - 1):
+        pack_sides(b)
+
     @pl.when(has_right)
     def _():
         to_right.start()
@@ -233,12 +276,15 @@
     @pl.when(jnp.logical_not(has_up))
     def _():
         top_in[...] = jnp.zeros_like(top_in)
-        corner_top[...] = jnp.zeros_like(corner_top)
 
     @pl.when(jnp.logical_not(has_down))
     def _():
         bot_in[...] = jnp.zeros_like(bot_in)
-        corner_bot[...] = jnp.zeros_like(corner_bot)
+
+    for k, (_, _, of) in enumerate(corners):
+        @pl.when(jnp.logical_not(of))
+        def _():
+            corner_in[k] = jnp.zeros((EDGE, LANES), F32)
 
     for slot, _, of, _, _ in peers:
         @pl.when(jnp.logical_not(of))
@@ -262,6 +308,7 @@
                 [(rows, pl.ds(pl.multiple_of(LANES + c * chunk, LANES), chunk))],
             )
 
+    forward(0)
     reach_in = (pair + 2) * LANES
     i = lax.broadcasted_iota(jnp.int32, (reach_in, pair * LANES), 0)
     j = lax.broadcasted_iota(jnp.int32, (reach_in, pair * LANES), 1) + LANES
@@ -295,20 +342,9 @@
         rows = pl.ds(b * 16, 16)
         lane = lax.broadcasted_iota(jnp.int32, (16, LANES), 1)
         pack = jnp.where(lane >= LANES // 2, left_in[rows, :], right_in[rows, :])
-        corner[rows, :] = pack
         put_split(split, decode(*edge_block(pack)), [(rows, lanes) for lanes in sides])
 
-    @pl.when(has_down)
-    def _():
-        corner_down.start()
-
-    @pl.when(has_up)
-    def _():
-        corner_up.start()
-
-    for i in range(early, len(pieces)):
-        send_piece(i)
-
+    forward(1)
     for j in sorted({0, tiles // pair - 1}):
         box_across(split, j, own)
 
@@ -345,6 +381,7 @@
         acc_g = part if acc_g is None else acc_g + part
     tab_out[:, 0:LANES] = jnp.sum(acc_g, 0, keepdims=True)
 
+    forward(2)
     sub = lax.broadcasted_iota(jnp.int32, (8, LANES), 0)
 
     def finish(t, top, bottom):
@@ -411,15 +448,14 @@
     done = 0
     for i, piece in enumerate(pieces):
         if i == 0:
-            @pl.when(has_up)
-            def _():
-                corner_down.wait_recv()
-
-            @pl.when(has_down)
-            def _():
-                corner_up.wait_recv()
-
-            put_halo([decode(*edge_block(pack[...])) for pack in (corner_top, corner_bot)], sides)
+            for copy, _, of in corners:
+                @pl.when(of)
+                def _():
+                    copy.wait_recv()
+
+            lane = lax.broadcasted_iota(jnp.int32, (EDGE, LANES), 1)
+            packs = [jnp.where(lane >= LANES // 2, corner_in[k], corner_in[k + 1]) for k in (0, 2)]
+            put_halo([decode(*edge_block(pack)) for pack in packs], sides)
 
         @pl.when(has_up)
         def _():
@@ -489,13 +525,22 @@
     def _():
         for copy in downs:
             copy.wait_send()
-        corner_down.wait_send()
 
     @pl.when(has_up)
     def _():
         for copy in ups:
             copy.wait_send()
-        corner_up.wait_send()
+
+    for copy, to, _ in corners:
+        @pl.when(to)
+        def _():
+            copy.wait_send()
+
+    for group in via:
+        for give, copy in group[2:]:
+            @pl.when(give)
+            def _():
+                copy.wait_send()
 
     @pl.when(has_right)
     def _():
@@ -511,11 +556,17 @@
             copy.wait_send()
 
 
-def back_kernel(n_rows, n_cols, block, gam, coh, memt, fit, ramped, coherence, out, across, sem):
+def back_kernel(n_rows, n_cols, block, gam, coh, memt, fit, ramped, coherence, out, across, lines, sem):
     height, width = coh.shape
     me_r, me_c = lax.axis_index("rows"), lax.axis_index("cols")
     coh_copy = pltpu.make_async_copy(coh, coherence, sem.at[0])
     coh_copy.start()
+    for g in range(height // 8):
+        row = lax.broadcasted_iota(jnp.int32, (8, LANES), 0) + (me_r * height + g * 8)
+        dv = (row.astype(F32) + 0.5) * (2.0 / (height * n_rows)) - 1.0 - fit[6:7, :]
+        one = memt[g * 8 : g * 8 + 8, :]
+        for m, value in enumerate((fit[0:1, :] + fit[4:5, :] * dv, fit[1:2, :] + fit[5:6, :] * dv, fit[2:3, :], fit[3:4, :])):
+            lines[g, m] = jnp.broadcast_to(row_sum(one * value), (8, LANES))
     lane_all = lax.broadcasted_iota(jnp.int32, (8, width), 1) + me_c * width
     across[...] = (lane_all.astype(F32) + 0.5) * (2.0 / (width * n_cols)) - 1.0
 
@@ -523,22 +574,16 @@
     for i in range(height // block):
         @pl.loop(0, block // 8)
         def _(b):
-            first = pl.multiple_of(i * block + b * 8, 8)
-            rows = pl.ds(first, 8)
-            row = lax.broadcasted_iota(jnp.int32, (8, LANES), 0) + (me_r * height + first)
-            v = (row.astype(F32) + 0.5) * (2.0 / (height * n_rows)) - 1.0
-            one = memt[rows, :]
-            dv = v - fit[6:7, :]
-            base_r = row_sum(one * (fit[0:1, :] + fit[4:5, :] * dv))
-            base_i = row_sum(one * (fit[1:2, :] + fit[5:6, :] * dv))
-            slope_r = row_sum(one * fit[2:3, :])
-            slope_i = row_sum(one * fit[3:4, :])
-            real, imag = gam[0, rows, :], gam[1, rows, :]
-            u = across[...]
-            model_real = base_r + slope_r * u
-            model_imag = base_i + slope_i * u
-            out[0, rows, :] = real * model_real + imag * model_imag
-            out[1, rows, :] = imag * model_real - real * model_imag
+            g = i * (block // 8) + b
+            rows = pl.ds(pl.multiple_of(g * 8, 8), 8)
+            base_r, base_i, slope_r, slope_i = [lines[g, m] for m in range(4)]
+            for t in range(width // LANES):
+                lanes = slice(t * LANES, (t + 1) * LANES)
+                real, imag, u = gam[0, rows, lanes], gam[1, rows, lanes], across[:, lanes]
+                model_real = base_r + slope_r * u
+                model_imag = base_i + slope_i * u
+                out[0, rows, lanes] = real * model_real + imag * model_imag
+                out[1, rows, lanes] = imag * model_real - real * model_imag
 
         rows = pl.ds(i * block, block)
         copy = pltpu.make_async_copy(out.at[:, rows, :], ramped.at[:, rows, :], sem.at[1 + i])
@@ -583,9 +628,8 @@
             pltpu.VMEM((height, LANES), F32),
             pltpu.VMEM((height, LANES), F32),
             pltpu.VMEM((height, LANES), F32),
-            pltpu.VMEM((height, LANES), F32),
-            pltpu.VMEM((EDGE, LANES), F32),
-            pltpu.VMEM((EDGE, LANES), F32),
+            pltpu.VMEM((3, EDGE, width), F32),
+            pltpu.VMEM((4, EDGE, LANES), F32),
             pltpu.VMEM((2, 4, height, wide), BF16),
             pltpu.VMEM((2, 4, 2 * EDGE, wide), BF16),
             pltpu.VMEM((4, height + 2 * EDGE, width), F32),
@@ -599,7 +643,8 @@
             dma((4, 3)),
             dma((2, pieces)), dma((2, pieces)),
             dma((2,)), dma((2,)),
-            dma((2,)), dma((2,)),
+            dma((4,)), dma((4,)),
+            dma((pieces,)), dma((pieces,)),
             dma((slots,)), dma((slots,)),
         ],
         compiler_params=pltpu.CompilerParams(
@@ -619,6 +664,7 @@
         scratch_shapes=[
             pltpu.VMEM((2, height, width), F32),
             pltpu.VMEM((8, width), F32),
+            pltpu.VMEM((height // 8, 4, 8, LANES), F32),
             dma((1 + height // block,)),
         ],
         compiler_params=pltpu.CompilerParams(vmem_limit_bytes=16 * 1024 * 1024),

time: 31.5 us -> 30.6 us (0.971)
  the two profiles are of different devices: /device:TPU:0 before, /device:TPU:11 now
where the time goes in v3:
time: 30.6 us; the launch traced here: 30.4 us
  Pallas kernels  29.8 us (97%)
  between operations  0.64 us (2%)
    pallas_call x1, Pallas kernels, on_device(): pl.pallas_call(functools.partial(front_kernel, n_rows, n_cols, reach), ou...  28.1 us
    pallas_call x1, Pallas kernels, on_device(): pl.pallas_call(functools.partial(back_kernel, n_rows, n_cols, block), out...  1.75 us

profile of v3, /device:TPU:11, one launch (start us, length us, event | category | flops | bytes accessed | tf_op | source)
XLA Modules:
  0.0 30.4 jit_solution(6493241657303444933)
XLA Ops:
  0.6 28.1 %front.1 = (f32[2,128,2048]{2,1,0:T(8,128)S(1)}, f32[128,2048]{1,0:T(8,128)S(1)}, f32[128,128]{1,0:T(8,128)S(1)}, f32[8,128]{1,0:T(8,128)S(1)}) custom-call(f32[2,128,2048]{2,1,0:T(8,128)} %lead.1, f32[2,128,2048]{2,1,0:T(8,128)} %trail.1, s32[128,2048]{1,0:T(8,128)} %flags.1, s32[1,128]{1,0:T(1,128)} %bitcast.1), custom_call_target="tpu_custom_call" | custom-call | tf_op jit(solution)/shard_map/front/pallas_call | solution.py:608
  28.7 1.7 %back.1 = (f32[2,128,2048]{2,1,0:T(8,128)}, f32[128,2048]{1,0:T(8,128)}) custom-call(f32[2,128,2048]{2,1,0:T(8,128)S(1)} %get-tuple-element.6.gam, f32[128,2048]{1,0:T(8,128)S(1)} %get-tuple-element.7.coh, f32[128,128]{1,0:T(8,128)S(1)} %get-tuple-element.8.memt, f32[8,128]{1,0:T(8,128)S(1)} %get-tuple-element.9.fit), custom_call_target="tpu_custom_call" | custom-call | tf_op jit(solution)/shard_map/back/pallas_call | solution.py:656

commit v4 on v3

--- a/solution.py
+++ b/solution.py
@@ -89,7 +89,7 @@
     relay_in, corner_in, split, halo_split, boxed, ribbon, across, row_parts, flag_parts, acc_h,
     tab_out, tab_in,
     load_sem, halo_send, halo_recv, side_send, side_recv, corner_send, corner_recv,
-    relay_send, relay_recv, tab_send, tab_recv,
+    relay_send, relay_recv, tab_send, tab_recv, token,
 ):
     me_r, me_c = lax.axis_index("rows"), lax.axis_index("cols")
     height, width = flags.shape
@@ -112,7 +112,7 @@
             copy.start()
         return group
 
-    loads = [load(0, pl.ds(low, EDGE)), load(1, pl.ds(0, EDGE)), load(2, pl.ds(EDGE, low - EDGE))]
+    loads = [load(0, pl.ds(low, EDGE)), load(1, pl.ds(0, EDGE))]
     sweep_load = pltpu.make_async_copy(sweep, sv, load_sem.at[3, 0])
     sweep_load.start()
 
@@ -125,12 +125,17 @@
             to = jnp.logical_and(me_r + dr >= 0, me_r + dr < n_rows)
             of = jnp.logical_and(me_r - dr >= 0, me_r - dr < n_rows)
             peers.append(((dr + reach) * n_cols + dc, to, of, me_r + dr, lax.rem(me_c + dc, n_cols)))
-    for _, to, _, row, col in peers:
+    near = reach == 1
+    n_greeted = 0
+    for slot, to, _, row, col in peers:
+        dr, dc = slot // n_cols - reach, slot % n_cols
+        if near and dr != 0 and dc != 0:
+            continue
+        n_greeted = n_greeted + to.astype(jnp.int32)
+
         @pl.when(to)
         def _():
             pl.semaphore_signal(barrier, inc=1, device_id=(row, col), device_id_type=MESH)
-
-    n_peers = (jnp.minimum(me_r, reach) + jnp.minimum(n_rows - 1 - me_r, reach) + 1) * n_cols - 1
 
     def remote(src, dst, send, recv, row, col):
         return pltpu.make_async_remote_copy(
@@ -219,77 +224,87 @@
 
     for copy in loads[0] + loads[1]:
         copy.wait()
+    loads.append(load(2, pl.ds(EDGE, low - EDGE)))
     for b in (0, height // 16 - 1):
         pack_sides(b)
     for piece in pieces:
         encode_rows(low, down_out, piece)
         encode_rows(0, up_out, piece)
 
-    pl.semaphore_wait(barrier, n_peers)
+    pl.semaphore_wait(barrier, n_greeted)
+    n_via = jnp.where(even, n_up, n_down)
+
+    def send(point):
+        slots = (0, 1) if point == 0 else (point + 1,)
+        for v in range(relayed + 1):
+            later = [i for i in range(v, len(pieces)) if point == (i + min(1, v) + (1 if i == v == 3 else 0) if v else i)]
+            for parity, straight, other, asked in ((even, downs, ups, 0), (odd, ups, downs, 1)):
+                @pl.when(parity & (n_via == v))
+                def _():
+                    far, near_by = (has_up, has_down) if asked == 0 else (has_down, has_up)
+                    for k in slots:
+                        if k < v:
+                            via[k][asked][1].start()
+                        elif k - v < len(pieces):
+                            @pl.when(near_by)
+                            def _():
+                                straight[k - v].start()
+                    for i in later:
+                        @pl.when(far)
+                        def _():
+                            other[i].start()
+
+    send(0)
+    if near:
+        for dc in range(1, n_cols):
+            pl.semaphore_signal(token, inc=1, device_id=(me_r, lax.rem(me_c + dc, n_cols)), device_id_type=MESH)
+
+    for copy in loads[2]:
+        copy.wait()
+
+    for b in range(1, height // 16 - 1):
+        pack_sides(b)
+
+    @pl.when(has_right)
+    def _():
+        to_right.start()
+
+    @pl.when(has_left)
+    def _():
+        to_left.start()
+
+    @pl.when(jnp.logical_not(has_left))
+    def _():
+        left_in[...] = jnp.zeros_like(left_in)
+
+    @pl.when(jnp.logical_not(has_right))
+    def _():
+        right_in[...] = jnp.zeros_like(right_in)
+
+    @pl.when(jnp.logical_not(has_up))
+    def _():
+        top_in[...] = jnp.zeros_like(top_in)
+
+    @pl.when(jnp.logical_not(has_down))
+    def _():
+        bot_in[...] = jnp.zeros_like(bot_in)
+
+    for k, (_, _, of) in enumerate(corners):
+        @pl.when(jnp.logical_not(of))
+        def _():
+            corner_in[k] = jnp.zeros((EDGE, LANES), F32)
+
+    for slot, _, of, _, _ in peers:
+        @pl.when(jnp.logical_not(of))
+        def _():
+            tab_in[slot] = jnp.zeros((1, 2 * LANES), F32)
+
+    if near:
+        pl.semaphore_wait(token, n_cols - 1)
     for copy, to, _ in corners:
         @pl.when(to)
         def _():
             copy.start()
-
-    for group in via:
-        for ask, copy in group[:2]:
-            @pl.when(ask)
-            def _():
-                copy.start()
-
-    for i in range(len(pieces)):
-        straight_down, straight_up = has_down, has_up
-        if i < relayed:
-            straight_down &= jnp.logical_not(via[i][1][0])
-            straight_up &= jnp.logical_not(via[i][0][0])
-
-        @pl.when(straight_down)
-        def _():
-            downs[i].start()
-
-        @pl.when(straight_up)
-        def _():
-            ups[i].start()
-
-    for copy in loads[2]:
-        copy.wait()
-
-    for b in range(1, height // 16 - 1):
-        pack_sides(b)
-
-    @pl.when(has_right)
-    def _():
-        to_right.start()
-
-    @pl.when(has_left)
-    def _():
-        to_left.start()
-
-    @pl.when(jnp.logical_not(has_left))
-    def _():
-        left_in[...] = jnp.zeros_like(left_in)
-
-    @pl.when(jnp.logical_not(has_right))
-    def _():
-        right_in[...] = jnp.zeros_like(right_in)
-
-    @pl.when(jnp.logical_not(has_up))
-    def _():
-        top_in[...] = jnp.zeros_like(top_in)
-
-    @pl.when(jnp.logical_not(has_down))
-    def _():
-        bot_in[...] = jnp.zeros_like(bot_in)
-
-    for k, (_, _, of) in enumerate(corners):
-        @pl.when(jnp.logical_not(of))
-        def _():
-            corner_in[k] = jnp.zeros((EDGE, LANES), F32)
-
-    for slot, _, of, _, _ in peers:
-        @pl.when(jnp.logical_not(of))
-        def _():
-            tab_in[slot] = jnp.zeros((1, 2 * LANES), F32)
 
     lane_all = lax.broadcasted_iota(jnp.int32, (8, width), 1) + me_c * width
     across[...] = (lane_all.astype(F32) + 0.5) * (2.0 / total_cols) - 1.0
@@ -308,26 +323,32 @@
                 [(rows, pl.ds(pl.multiple_of(LANES + c * chunk, LANES), chunk))],
             )
 
-    forward(0)
+    send(1)
     reach_in = (pair + 2) * LANES
     i = lax.broadcasted_iota(jnp.int32, (reach_in, pair * LANES), 0)
     j = lax.broadcasted_iota(jnp.int32, (reach_in, pair * LANES), 1) + LANES
     ribbon[...] = jnp.logical_and(i >= j - SIDE, i < j + SIDE).astype(F32).astype(BF16)
 
-    def box_across(source, j, targets):
+    def box_across(j):
         inner = pl.ds(pl.multiple_of(j * pair * LANES, pair * LANES), reach_in)
         outer = pl.ds(pl.multiple_of(j * pair * LANES, pair * LANES), pair * LANES)
         for plane in range(4):
-            sums = jnp.dot(source[0, plane, :, inner], ribbon[...], preferred_element_type=F32)
-            sums = sums + jnp.dot(source[1, plane, :, inner], ribbon[...], preferred_element_type=F32)
-            for first, target, count in targets:
-                boxed[plane, target : target + count, outer] = sums[first : first + count]
-
-    own = [(0, EDGE, height)]
-
-    @pl.loop(1, max(1, tiles // pair - 1))
+            sums = jnp.dot(split[0, plane, :, inner], ribbon[...], preferred_element_type=F32)
+            sums = sums + jnp.dot(split[1, plane, :, inner], ribbon[...], preferred_element_type=F32)
+            boxed[plane, EDGE : EDGE + height, outer] = sums
+
+    last = tiles // pair - 1
+    middle = max(1, tiles // pair // 2)
+
+    @pl.loop(1, middle)
     def _(j):
-        box_across(split, j, own)
+        box_across(j)
+
+    send(2)
+
+    @pl.loop(middle, max(middle, last))
+    def _(j):
+        box_across(j)
 
     @pl.when(has_left)
     def _():
@@ -344,9 +365,11 @@
         pack = jnp.where(lane >= LANES // 2, left_in[rows, :], right_in[rows, :])
         put_split(split, decode(*edge_block(pack)), [(rows, lanes) for lanes in sides])
 
+    send(3)
+    forward(0)
     forward(1)
-    for j in sorted({0, tiles // pair - 1}):
-        box_across(split, j, own)
+    for j in sorted({0, last}):
+        box_across(j)
 
     sweep_load.wait()
     kind = lax.rem(lax.broadcasted_iota(jnp.int32, (LANES, height), 0), SWEEP_TALLY)
@@ -381,7 +404,7 @@
         acc_g = part if acc_g is None else acc_g + part
     tab_out[:, 0:LANES] = jnp.sum(acc_g, 0, keepdims=True)
 
-    forward(2)
+    send(4)
     sub = lax.broadcasted_iota(jnp.int32, (8, LANES), 0)
 
     def finish(t, top, bottom):
@@ -434,17 +457,42 @@
 
     edge_groups, groups = EDGE // 8, height // 8
 
-    @pl.loop(0, tiles)
+    @pl.loop(0, tiles // 2)
     def _(t):
         finish(t, edge_groups, groups - edge_groups)
 
+    send(5)
+    forward(2)
+
+    @pl.loop(tiles // 2, tiles)
+    def _(t):
+        finish(t, edge_groups, groups - edge_groups)
+
+    send(6)
+
     acc_h[...] = add_rows(range(edge_groups, groups - edge_groups))
 
     def put_halo(sources, where):
         for part, products in enumerate(sources):
-            put_split(halo_split, products, [(pl.ds(part * EDGE, EDGE), lanes) for lanes in where])
-
-    beyond = [(0, 0, EDGE), (EDGE, EDGE + height, EDGE)]
+            for plane, value in enumerate(products):
+                first = (plane * 2 + part) * EDGE
+                high = value.astype(BF16)
+                low_part = (value - high.astype(F32)).astype(BF16)
+                for lanes in where:
+                    halo_split[first : first + EDGE, lanes] = high
+                    halo_split[8 * EDGE + first : 9 * EDGE + first, lanes] = low_part
+
+    def box_halo(j):
+        inner = pl.ds(j * pair * LANES, reach_in)
+        outer = pl.ds(j * pair * LANES, pair * LANES)
+        sums = jnp.dot(halo_split[:, inner], ribbon[...], preferred_element_type=F32)
+        for plane in range(4):
+            for part, target in enumerate((0, EDGE + height)):
+                first = (plane * 2 + part) * EDGE
+                boxed[plane, target : target + EDGE, outer] = (
+                    sums[first : first + EDGE] + sums[8 * EDGE + first : 9 * EDGE + first]
+                )
+
     done = 0
     for i, piece in enumerate(pieces):
         if i == 0:
@@ -470,12 +518,13 @@
         put_halo([decode(*[halo[m, :, source] for m in range(3)]) for halo in (top_in, bot_in)], [target])
         ready = tiles // pair if i == len(pieces) - 1 else max(0, (piece[1] - 1) // pair)
         for j in range(done, ready):
-            box_across(halo_split, j, beyond)
+            box_halo(j)
         if ready > done:
-            @pl.loop(done * pair, ready * pair)
-            def _(t):
-                finish(t, 0, edge_groups)
-                finish(t, groups - edge_groups, groups)
+            @pl.loop(done, ready)
+            def _(j):
+                for t in range(pair):
+                    finish(j * pair + t, 0, edge_groups)
+                    finish(j * pair + t, groups - edge_groups, groups)
         done = ready
 
     acc_last = acc_h[...] + add_rows(list(range(edge_groups)) + list(range(groups - edge_groups, groups)))
@@ -631,7 +680,7 @@
             pltpu.VMEM((3, EDGE, width), F32),
             pltpu.VMEM((4, EDGE, LANES), F32),
             pltpu.VMEM((2, 4, height, wide), BF16),
-            pltpu.VMEM((2, 4, 2 * EDGE, wide), BF16),
+            pltpu.VMEM((16 * EDGE, wide), BF16),
             pltpu.VMEM((4, height + 2 * EDGE, width), F32),
             pltpu.VMEM(((pair + 2) * LANES, pair * LANES), BF16),
             pltpu.VMEM((8, width), F32),
@@ -646,6 +695,7 @@
             dma((4,)), dma((4,)),
             dma((pieces,)), dma((pieces,)),
             dma((slots,)), dma((slots,)),
+            pltpu.SemaphoreType.REGULAR,
         ],
         compiler_params=pltpu.CompilerParams(
             collective_id=0, has_side_effects=True, vmem_limit_bytes=60 * 1024 * 1024

time: 30.6 us -> 27.8 us (0.908)
  the two profiles are of different devices: /device:TPU:11 before, /device:TPU:0 now
where the time goes in v4:
time: 27.8 us; the launch traced here: 27.6 us
  Pallas kernels  27 us (97%)
  between operations  0.64 us (2%)
    pallas_call x1, Pallas kernels, on_device(): pl.pallas_call(functools.partial(front_kernel, n_rows, n_cols, reach), ou...  25.2 us
    pallas_call x1, Pallas kernels, on_device(): pl.pallas_call(functools.partial(back_kernel, n_rows, n_cols, block), out...  1.75 us

profile of v4, /device:TPU:0, one launch (start us, length us, event | category | flops | bytes accessed | tf_op | source)
XLA Modules:
  0.0 27.6 jit_solution(18402237668585302184)
XLA Ops:
  0.6 25.2 %front.1 = (f32[2,128,2048]{2,1,0:T(8,128)S(1)}, f32[128,2048]{1,0:T(8,128)S(1)}, f32[128,128]{1,0:T(8,128)S(1)}, f32[8,128]{1,0:T(8,128)S(1)}) custom-call(f32[2,128,2048]{2,1,0:T(8,128)} %lead.1, f32[2,128,2048]{2,1,0:T(8,128)} %trail.1, s32[128,2048]{1,0:T(8,128)} %flags.1, s32[1,128]{1,0:T(1,128)} %bitcast.1), custom_call_target="tpu_custom_call" | custom-call | tf_op jit(solution)/shard_map/front/pallas_call | solution.py:657
  25.9 1.7 %back.1 = (f32[2,128,2048]{2,1,0:T(8,128)}, f32[128,2048]{1,0:T(8,128)}) custom-call(f32[2,128,2048]{2,1,0:T(8,128)S(1)} %get-tuple-element.6.gam, f32[128,2048]{1,0:T(8,128)S(1)} %get-tuple-element.7.coh, f32[128,128]{1,0:T(8,128)S(1)} %get-tuple-element.8.memt, f32[8,128]{1,0:T(8,128)S(1)} %get-tuple-element.9.fit), custom_call_target="tpu_custom_call" | custom-call | tf_op jit(solution)/shard_map/back/pallas_call | solution.py:706

commit v5 on v4

--- a/solution.py
+++ b/solution.py
@@ -64,10 +64,11 @@
 
 
 def cuts(tiles):
-    if tiles < 8:
-        return ((0, tiles),)
-    marks = [0, tiles // 4, tiles // 2, tiles * 3 // 4, tiles - 1, tiles]
-    return tuple(zip(marks[:-1], marks[1:]))
+    if tiles < EDGE:
+        return ((0, tiles),), ((0, tiles),), ((1, 1),)
+    down = [mark * tiles // 16 for mark in (0, 3, 7, 11, 14, 16)]
+    up = [mark * tiles // 16 for mark in (0, 5, 9, 13)] + [tiles - 1]
+    return tuple(zip(down[:-1], down[1:])), tuple(zip(up[:-1], up[1:])), ((2, 1), (3, 2), (4, 3), (5, 4))
 
 
 def fold(x):
@@ -86,7 +87,7 @@
     lead, trail, flags, sweep,
     gam, coh, memt, fit,
     av, bv, wv, sv, up_out, down_out, top_in, bot_in, left_out, right_out, left_in, right_in,
-    relay_in, corner_in, split, halo_split, boxed, ribbon, across, row_parts, flag_parts, acc_h,
+    relay_in, corner_in, split, halo_split, boxed, ribbon, across, own_part, row_parts, flag_parts, acc_h,
     tab_out, tab_in,
     load_sem, halo_send, halo_recv, side_send, side_recv, corner_send, corner_recv,
     relay_send, relay_recv, tab_send, tab_recv, token,
@@ -99,21 +100,36 @@
     chunk = 512 if width % 512 == 0 else LANES
     has_up, has_down = me_r > 0, me_r < n_rows - 1
     has_left, has_right = me_c > 0, me_c < n_cols - 1
-    pieces = cuts(tiles)
+    down_cuts, up_cuts, steps = cuts(tiles)
     pair = 2 if tiles % 2 == 0 else 1
 
-    def load(part, rows):
+    def load(part, rows, lanes=pl.ds(0, width)):
         group = [
-            pltpu.make_async_copy(lead.at[:, rows, :], av.at[:, rows, :], load_sem.at[part, 0]),
-            pltpu.make_async_copy(trail.at[:, rows, :], bv.at[:, rows, :], load_sem.at[part, 1]),
-            pltpu.make_async_copy(flags.at[rows, :], wv.at[rows, :], load_sem.at[part, 2]),
+            pltpu.make_async_copy(lead.at[:, rows, lanes], av.at[:, rows, lanes], load_sem.at[part, 0]),
+            pltpu.make_async_copy(trail.at[:, rows, lanes], bv.at[:, rows, lanes], load_sem.at[part, 1]),
+            pltpu.make_async_copy(flags.at[rows, lanes], wv.at[rows, lanes], load_sem.at[part, 2]),
         ]
         for copy in group:
             copy.start()
         return group
 
-    loads = [load(0, pl.ds(low, EDGE)), load(1, pl.ds(0, EDGE))]
-    sweep_load = pltpu.make_async_copy(sweep, sv, load_sem.at[3, 0])
+    top_rows, low_rows = pl.ds(0, EDGE), pl.ds(low, EDGE)
+    tucked = up_cuts[-1][1] == tiles - 1
+    first = max(up_cuts[:2][-1][1], down_cuts[:3][-1][1]) * LANES
+    loads = [load(0, top_rows, pl.ds(0, first))]
+    if first < width:
+        if tucked:
+            loads.append(load(1, top_rows, pl.ds(width - LANES, LANES)))
+        loads.append(load(2, low_rows, pl.ds(0, first)))
+    later_loads = []
+    if first < width:
+        rest = width - first - (LANES if tucked else 0)
+        if rest:
+            later_loads.append(load(3, top_rows, pl.ds(first, rest)))
+        later_loads.append(load(4, low_rows, pl.ds(first, width - first)))
+    else:
+        later_loads.append(load(4, low_rows))
+    sweep_load = pltpu.make_async_copy(sweep, sv, load_sem.at[6, 0])
     sweep_load.start()
 
     barrier = pltpu.get_barrier_semaphore()
@@ -147,15 +163,14 @@
 
     downs = [
         remote(cut(down_out, p), cut(top_in, p), halo_send.at[0, i], halo_recv.at[0, i], me_r + 1, me_c)
-        for i, p in enumerate(pieces)
+        for i, p in enumerate(down_cuts)
     ]
     ups = [
         remote(cut(up_out, p), cut(bot_in, p), halo_send.at[1, i], halo_recv.at[1, i], me_r - 1, me_c)
-        for i, p in enumerate(pieces)
+        for i, p in enumerate(up_cuts)
     ]
     to_right = remote(right_out, left_in, side_send.at[0], side_recv.at[0], me_r, me_c + 1)
     to_left = remote(left_out, right_in, side_send.at[1], side_recv.at[1], me_r, me_c - 1)
-    top_rows, low_rows = pl.ds(0, EDGE), pl.ds(low, EDGE)
     corners = []
     for k, (src, rows, dr, dc, to, of) in enumerate((
         (right_out, low_rows, 1, 1, has_down & has_right, has_up & has_left),
@@ -166,7 +181,7 @@
         copy = remote(src.at[rows], corner_in.at[k], corner_send.at[k], corner_recv.at[k], me_r + dr, me_c + dc)
         corners.append((copy, to, of))
 
-    relayed = len(pieces) - 2 if n_rows % 2 == 0 and n_rows > 2 and len(pieces) > 2 else 0
+    relayed = 3 if n_rows % 2 == 0 and n_rows > 2 and len(up_cuts) > 3 else 0
     odd = lax.rem(me_r, 2) == 1
     even = jnp.logical_not(odd)
     place = lax.div(me_r, 2) * 4
@@ -174,23 +189,23 @@
     n_down = jnp.minimum(relayed, 4 - lax.div(place + 4, n_rows // 2)) if relayed else 0
     via = []
     for i in range(relayed):
-        p = pieces[i]
+        p, q = up_cuts[i], down_cuts[i]
         ask_up, ask_down = even & (n_up > i), odd & (n_down > i)
         give_up, give_down = odd & (n_up > i), even & (n_down > i)
         via.append((
             (ask_up, remote(cut(up_out, p), cut(relay_in, p), halo_send.at[1, i], relay_recv.at[i], me_r + 1, me_c)),
-            (ask_down, remote(cut(down_out, p), cut(relay_in, p), halo_send.at[0, i], relay_recv.at[i], me_r - 1, me_c)),
+            (ask_down, remote(cut(down_out, q), cut(relay_in, q), halo_send.at[0, i], relay_recv.at[i], me_r - 1, me_c)),
             (give_up, remote(cut(relay_in, p), cut(bot_in, p), relay_send.at[i], halo_recv.at[1, i], me_r - 2, me_c)),
-            (give_down, remote(cut(relay_in, p), cut(top_in, p), relay_send.at[i], halo_recv.at[0, i], me_r + 2, me_c)),
+            (give_down, remote(cut(relay_in, q), cut(top_in, q), relay_send.at[i], halo_recv.at[0, i], me_r + 2, me_c)),
         ))
 
     def forward(i):
         if i >= relayed:
             return
-        for give, copy in via[i][2:]:
+        for (_, arrival), (give, copy) in zip(via[i][:2], via[i][2:]):
             @pl.when(give)
             def _():
-                via[i][0][1].wait_recv()
+                arrival.wait_recv()
                 copy.start()
 
     def encode_rows(first, out, piece):
@@ -222,34 +237,48 @@
             ),
         )
 
-    for copy in loads[0] + loads[1]:
-        copy.wait()
-    loads.append(load(2, pl.ds(EDGE, low - EDGE)))
-    for b in (0, height // 16 - 1):
-        pack_sides(b)
-    for piece in pieces:
+    for group in loads:
+        for copy in group:
+            copy.wait()
+
+    def tuck(piece):
+        if tucked:
+            for t in range(piece[0], min(piece[1], EDGE - 1)):
+                for k in range(3):
+                    up_out[k, EDGE - 1 : EDGE, t * LANES : (t + 1) * LANES] = up_out[k, t : t + 1, width - LANES : width]
+
+    if first == width:
+        for copy in later_loads[0]:
+            copy.wait()
+    if tucked:
+        encode_rows(0, up_out, (tiles - 1, tiles))
+    for piece in up_cuts[:2]:
+        encode_rows(0, up_out, piece)
+        tuck(piece)
+    for piece in down_cuts[:3]:
         encode_rows(low, down_out, piece)
-        encode_rows(0, up_out, piece)
 
     pl.semaphore_wait(barrier, n_greeted)
     n_via = jnp.where(even, n_up, n_down)
 
     def send(point):
-        slots = (0, 1) if point == 0 else (point + 1,)
         for v in range(relayed + 1):
-            later = [i for i in range(v, len(pieces)) if point == (i + min(1, v) + (1 if i == v == 3 else 0) if v else i)]
+            later = [i for i in range(v, len(down_cuts)) if point == (i + 3 if v else i)]
             for parity, straight, other, asked in ((even, downs, ups, 0), (odd, ups, downs, 1)):
+                ahead = 2 if v == asked == 0 else 1
+                slots = range(ahead + 1) if point == 0 else (point + ahead,)
+
                 @pl.when(parity & (n_via == v))
                 def _():
                     far, near_by = (has_up, has_down) if asked == 0 else (has_down, has_up)
                     for k in slots:
                         if k < v:
                             via[k][asked][1].start()
-                        elif k - v < len(pieces):
+                        elif k - v < len(straight):
                             @pl.when(near_by)
                             def _():
                                 straight[k - v].start()
-                    for i in later:
+                    for i in (i for i in later if i < len(other)):
                         @pl.when(far)
                         def _():
                             other[i].start()
@@ -259,7 +288,19 @@
         for dc in range(1, n_cols):
             pl.semaphore_signal(token, inc=1, device_id=(me_r, lax.rem(me_c + dc, n_cols)), device_id_type=MESH)
 
-    for copy in loads[2]:
+    if first < width:
+        for group in later_loads:
+            for copy in group:
+                copy.wait()
+        for piece in up_cuts[2:]:
+            encode_rows(0, up_out, piece)
+            tuck(piece)
+        for piece in down_cuts[3:]:
+            encode_rows(low, down_out, piece)
+    bulk = load(5, pl.ds(EDGE, low - EDGE))
+    for b in (0, height // 16 - 1):
+        pack_sides(b)
+    for copy in bulk:
         copy.wait()
 
     for b in range(1, height // 16 - 1):
@@ -407,44 +448,70 @@
     send(4)
     sub = lax.broadcasted_iota(jnp.int32, (8, LANES), 0)
 
-    def finish(t, top, bottom):
+    edge_groups, groups = EDGE // 8, height // 8
+
+    def shifted(x, following):
+        n1, n2, n4 = following if following else (None, None, None)
+        r1 = pltpu.roll(x, 7, 0)
+        y1 = x + (r1 if n1 is None else jnp.where(sub < 7, r1, n1))
+        r2 = pltpu.roll(y1, 6, 0)
+        y2 = y1 + (r2 if n2 is None else jnp.where(sub < 6, r2, n2))
+        r4 = pltpu.roll(y2, 4, 0)
+        return y2 + (r4 if n4 is None else jnp.where(sub < 4, r4, n4)), (r1, r2, r4)
+
+    def emit(g, lanes, window):
+        rows = slice(g * 8, g * 8 + 8)
+        inverse = lax.rsqrt((window[2] + 1.0) * (window[3] + 1.0))
+        real, imag = window[0] * inverse, window[1] * inverse
+        gam[0, rows, lanes] = real
+        gam[1, rows, lanes] = imag
+        coh[rows, lanes] = jnp.sqrt(real * real + imag * imag)
+        w, u = wv[rows, lanes].astype(F32), across[:, lanes]
+        wr, wi = w * real, w * imag
+        for m, value in enumerate((wr, wi, wr * u, wi * u)):
+            row_parts[g, m] += value
+
+    def group_rows(g):
+        return slice(g * 8, g * 8 + 8)
+
+    def finish(t):
         lanes = pl.ds(pl.multiple_of(t * LANES, LANES), LANES)
-        u = across[:, lanes]
-        state = [None] * 4
-        for g in range(bottom + 3, top - 1, -1):
-            window = []
+        eights = [[None] * 4 for _ in range(groups + 2)]
+        pairs = [[None] * 4 for _ in range(groups + 2)]
+        following = [None] * 4
+        for g in range(groups + 1, edge_groups - 1, -1):
             for plane in range(4):
-                x = boxed[plane, g * 8 : g * 8 + 8, lanes]
-                r1 = pltpu.roll(x, 7, 0)
-                if state[plane] is None:
-                    state[plane] = (r1, None, None, None, None, None)
-                    y1 = x + r1
-                    r2 = pltpu.roll(y1, 6, 0)
-                    y2 = y1 + r2
-                    r4 = pltpu.roll(y2, 4, 0)
-                    state[plane] = (r1, r2, r4, None, None, None)
-                    continue
-                n1, n2, n4, last, pair1, pair2 = state[plane]
-                y1 = x + jnp.where(sub < 7, r1, n1)
-                r2 = pltpu.roll(y1, 6, 0)
-                y2 = y1 + jnp.where(sub < 6, r2, n2)
-                r4 = pltpu.roll(y2, 4, 0)
-                y4 = y2 + jnp.where(sub < 4, r4, n4)
-                both = None if last is None else y4 + last
-                window.append(None if pair2 is None else both + pair2)
-                state[plane] = (r1, r2, r4, y4, both, pair1)
-            if len(window) < 4 or window[0] is None:
-                continue
-            rows = slice(g * 8, g * 8 + 8)
-            inverse = lax.rsqrt((window[2] + 1.0) * (window[3] + 1.0))
-            real, imag = window[0] * inverse, window[1] * inverse
-            gam[0, rows, lanes] = real
-            gam[1, rows, lanes] = imag
-            coh[rows, lanes] = jnp.sqrt(real * real + imag * imag)
-            w = wv[rows, lanes].astype(F32)
-            wr, wi = w * real, w * imag
-            for m, value in enumerate((wr, wi, wr * u, wi * u)):
-                row_parts[g, m] += value
+                eights[g][plane], following[plane] = shifted(boxed[plane, group_rows(g), lanes], following[plane])
+                if g <= groups - 1:
+                    pairs[g][plane] = eights[g][plane] + eights[g + 1][plane]
+            if g <= groups - 3:
+                emit(g, lanes, [pairs[g][p] + pairs[g + 2][p] for p in range(4)])
+        for p in range(4):
+            kept = (
+                pairs[edge_groups][p], eights[edge_groups][p] + pairs[edge_groups + 1][p], *following[p],
+                eights[groups - 2][p] + pairs[groups - 1][p], pairs[groups - 1][p],
+            )
+            for k, value in enumerate(kept):
+                own_part[p, k, :, lanes] = value
+
+    def finish_edges(t):
+        lanes = pl.ds(pl.multiple_of(t * LANES, LANES), LANES)
+        outer, inner = [None] * 4, [None] * 4
+        for p in range(4):
+            near, following = shifted(boxed[p, group_rows(1), lanes], [own_part[p, k, :, lanes] for k in (2, 3, 4)])
+            far, _ = shifted(boxed[p, group_rows(0), lanes], following)
+            inner[p] = near + own_part[p, 1, :, lanes]
+            outer[p] = far + near + own_part[p, 0, :, lanes]
+        emit(0, lanes, outer)
+        emit(1, lanes, inner)
+        for p in range(4):
+            _, following = shifted(boxed[p, group_rows(groups + 3), lanes], None)
+            far, following = shifted(boxed[p, group_rows(groups + 2), lanes], following)
+            near, _ = shifted(boxed[p, group_rows(groups + 1), lanes], following)
+            inner[p] = near + own_part[p, 5, :, lanes]
+            outer[p] = near + far + own_part[p, 6, :, lanes]
+        emit(groups - 2, lanes, inner)
+        emit(groups - 1, lanes, outer)
 
     def add_rows(groups):
         total = None
@@ -455,32 +522,29 @@
             total = part if total is None else total + part
         return total
 
-    edge_groups, groups = EDGE // 8, height // 8
-
     @pl.loop(0, tiles // 2)
     def _(t):
-        finish(t, edge_groups, groups - edge_groups)
+        finish(t)
 
     send(5)
     forward(2)
 
     @pl.loop(tiles // 2, tiles)
     def _(t):
-        finish(t, edge_groups, groups - edge_groups)
+        finish(t)
 
     send(6)
 
     acc_h[...] = add_rows(range(edge_groups, groups - edge_groups))
 
-    def put_halo(sources, where):
-        for part, products in enumerate(sources):
-            for plane, value in enumerate(products):
-                first = (plane * 2 + part) * EDGE
-                high = value.astype(BF16)
-                low_part = (value - high.astype(F32)).astype(BF16)
-                for lanes in where:
-                    halo_split[first : first + EDGE, lanes] = high
-                    halo_split[8 * EDGE + first : 9 * EDGE + first, lanes] = low_part
+    def put_halo(part, products, where):
+        for plane, value in enumerate(products):
+            first = (plane * 2 + part) * EDGE
+            high = value.astype(BF16)
+            low_part = (value - high.astype(F32)).astype(BF16)
+            for lanes in where:
+                halo_split[first : first + EDGE, lanes] = high
+                halo_split[8 * EDGE + first : 9 * EDGE + first, lanes] = low_part
 
     def box_halo(j):
         inner = pl.ds(j * pair * LANES, reach_in)
@@ -494,7 +558,8 @@
                 )
 
     done = 0
-    for i, piece in enumerate(pieces):
+    had_down, had_up = 0, 0
+    for i, (need_down, need_up) in enumerate(steps):
         if i == 0:
             for copy, _, of in corners:
                 @pl.when(of)
@@ -503,29 +568,42 @@
 
             lane = lax.broadcasted_iota(jnp.int32, (EDGE, LANES), 1)
             packs = [jnp.where(lane >= LANES // 2, corner_in[k], corner_in[k + 1]) for k in (0, 2)]
-            put_halo([decode(*edge_block(pack)) for pack in packs], sides)
+            for part, pack in enumerate(packs):
+                put_halo(part, decode(*edge_block(pack)), sides)
 
         @pl.when(has_up)
         def _():
-            downs[i].wait_recv()
+            for copy in downs[had_down:need_down]:
+                copy.wait_recv()
 
         @pl.when(has_down)
         def _():
-            ups[i].wait_recv()
-
-        source = pl.ds(piece[0] * LANES, (piece[1] - piece[0]) * LANES)
-        target = pl.ds((piece[0] + 1) * LANES, (piece[1] - piece[0]) * LANES)
-        put_halo([decode(*[halo[m, :, source] for m in range(3)]) for halo in (top_in, bot_in)], [target])
-        ready = tiles // pair if i == len(pieces) - 1 else max(0, (piece[1] - 1) // pair)
+            for copy in ups[had_up:need_up]:
+                copy.wait_recv()
+
+        end_up = up_cuts[need_up - 1][1]
+        if tucked and i == len(steps) - 1:
+            end_up = tiles
+            for t in range(EDGE - 1):
+                for k in range(3):
+                    bot_in[k, t : t + 1, width - LANES : width] = bot_in[k, EDGE - 1 : EDGE, t * LANES : (t + 1) * LANES]
+        ranges = ((down_cuts[had_down][0], down_cuts[need_down - 1][1]), (up_cuts[had_up][0], end_up))
+        for part, (halo, (start, end)) in enumerate(zip((top_in, bot_in), ranges)):
+            source = pl.ds(start * LANES, (end - start) * LANES)
+            target = pl.ds((start + 1) * LANES, (end - start) * LANES)
+            put_halo(part, decode(*[halo[m, :, source] for m in range(3)]), [target])
+        had_down, had_up = need_down, need_up
+        ready = tiles // pair if i == len(steps) - 1 else max(0, (min(ranges[0][1], ranges[1][1]) - 1) // pair)
         for j in range(done, ready):
             box_halo(j)
         if ready > done:
             @pl.loop(done, ready)
             def _(j):
                 for t in range(pair):
-                    finish(j * pair + t, 0, edge_groups)
-                    finish(j * pair + t, groups - edge_groups, groups)
+                    finish_edges(j * pair + t)
         done = ready
+        if i == 0:
+            send(7)
 
     acc_last = acc_h[...] + add_rows(list(range(edge_groups)) + list(range(groups - edge_groups, groups)))
     tab_out[:, LANES:] = jnp.sum(acc_last, 0, keepdims=True)
@@ -539,6 +617,35 @@
             copy.start()
 
     tab_in[reach * n_cols] = tab_out[...]
+    @pl.when(has_down)
+    def _():
+        for copy in downs:
+            copy.wait_send()
+
+    @pl.when(has_up)
+    def _():
+        for copy in ups:
+            copy.wait_send()
+
+    for copy, to, _ in corners:
+        @pl.when(to)
+        def _():
+            copy.wait_send()
+
+    for group in via:
+        for give, copy in group[2:]:
+            @pl.when(give)
+            def _():
+                copy.wait_send()
+
+    @pl.when(has_right)
+    def _():
+        to_right.wait_send()
+
+    @pl.when(has_left)
+    def _():
+        to_left.wait_send()
+
     for copy, _, of in swaps:
         @pl.when(of)
         def _():
@@ -570,35 +677,6 @@
     for m, value in enumerate(rows_out):
         fit[m : m + 1, :] = jnp.where(valid, value, 0.0)
 
-    @pl.when(has_down)
-    def _():
-        for copy in downs:
-            copy.wait_send()
-
-    @pl.when(has_up)
-    def _():
-        for copy in ups:
-            copy.wait_send()
-
-    for copy, to, _ in corners:
-        @pl.when(to)
-        def _():
-            copy.wait_send()
-
-    for group in via:
-        for give, copy in group[2:]:
-            @pl.when(give)
-            def _():
-                copy.wait_send()
-
-    @pl.when(has_right)
-    def _():
-        to_right.wait_send()
-
-    @pl.when(has_left)
-    def _():
-        to_left.wait_send()
-
     for copy, to, _ in swaps:
         @pl.when(to)
         def _():
@@ -649,7 +727,7 @@
     longest = 2 * height * n_rows // SWEEP_TALLY
     reach = max(1, min(n_rows - 1, (longest - 2) // height + 1))
     slots = (2 * reach + 1) * n_cols
-    pieces = len(cuts(width // LANES))
+    pieces = len(cuts(width // LANES)[0])
     pair = 2 if width // LANES % 2 == 0 else 1
     hbm = pl.BlockSpec(memory_space=pltpu.HBM)
     vmem = pl.BlockSpec(memory_space=pltpu.VMEM)
@@ -684,12 +762,13 @@
             pltpu.VMEM((4, height + 2 * EDGE, width), F32),
             pltpu.VMEM(((pair + 2) * LANES, pair * LANES), BF16),
             pltpu.VMEM((8, width), F32),
+            pltpu.VMEM((4, 7, 8, width), F32),
             pltpu.VMEM((height // 8, 4, 8, LANES), F32),
             pltpu.VMEM((height // 8, 3, 8, LANES), F32),
             pltpu.VMEM((8, LANES), F32),
             pltpu.VMEM((1, 2 * LANES), F32),
             pltpu.VMEM((slots, 1, 2 * LANES), F32),
-            dma((4, 3)),
+            dma((7, 3)),
             dma((2, pieces)), dma((2, pieces)),
             dma((2,)), dma((2,)),
             dma((4,)), dma((4,)),

time: 27.8 us -> 27.4 us (0.986)
  the two profiles are of different devices: /device:TPU:0 before, /device:TPU:19 now
where the time goes in v5:
time: 27.4 us; the launch traced here: 27.2 us
  Pallas kernels  26.6 us (97%)
  between operations  0.64 us (2%)
    pallas_call x1, Pallas kernels, on_device(): pl.pallas_call(functools.partial(front_kernel, n_rows, n_cols, reach), ou...  24.8 us
    pallas_call x1, Pallas kernels, on_device(): pl.pallas_call(functools.partial(back_kernel, n_rows, n_cols, block), out...  1.75 us

profile of v5, /device:TPU:19, one launch (start us, length us, event | category | flops | bytes accessed | tf_op | source)
XLA Modules:
  0.0 27.2 jit_solution(13683669005226037386)
XLA Ops:
  0.6 24.8 %front.1 = (f32[2,128,2048]{2,1,0:T(8,128)S(1)}, f32[128,2048]{1,0:T(8,128)S(1)}, f32[128,128]{1,0:T(8,128)S(1)}, f32[8,128]{1,0:T(8,128)S(1)}) custom-call(f32[2,128,2048]{2,1,0:T(8,128)} %lead.1, f32[2,128,2048]{2,1,0:T(8,128)} %trail.1, s32[128,2048]{1,0:T(8,128)} %flags.1, s32[1,128]{1,0:T(1,128)} %bitcast.1), custom_call_target="tpu_custom_call" | custom-call | tf_op jit(solution)/shard_map/front/pallas_call | solution.py:735
  25.5 1.7 %back.1 = (f32[2,128,2048]{2,1,0:T(8,128)}, f32[128,2048]{1,0:T(8,128)}) custom-call(f32[2,128,2048]{2,1,0:T(8,128)S(1)} %get-tuple-element.6.gam, f32[128,2048]{1,0:T(8,128)S(1)} %get-tuple-element.7.coh, f32[128,128]{1,0:T(8,128)S(1)} %get-tuple-element.8.memt, f32[8,128]{1,0:T(8,128)S(1)} %get-tuple-element.9.fit), custom_call_target="tpu_custom_call" | custom-call | tf_op jit(solution)/shard_map/back/pallas_call | solution.py:785

commit v6 on v5

--- a/solution.py
+++ b/solution.py
@@ -87,7 +87,7 @@
     lead, trail, flags, sweep,
     gam, coh, memt, fit,
     av, bv, wv, sv, up_out, down_out, top_in, bot_in, left_out, right_out, left_in, right_in,
-    relay_in, corner_in, split, halo_split, boxed, ribbon, across, own_part, row_parts, flag_parts, acc_h,
+    relay_in, corner_out, corner_in, split, halo_split, boxed, ribbon, across, own_part, row_parts, flag_parts, acc_h,
     tab_out, tab_in,
     load_sem, halo_send, halo_recv, side_send, side_recv, corner_send, corner_recv,
     relay_send, relay_recv, tab_send, tab_recv, token,
@@ -172,13 +172,13 @@
     to_right = remote(right_out, left_in, side_send.at[0], side_recv.at[0], me_r, me_c + 1)
     to_left = remote(left_out, right_in, side_send.at[1], side_recv.at[1], me_r, me_c - 1)
     corners = []
-    for k, (src, rows, dr, dc, to, of) in enumerate((
-        (right_out, low_rows, 1, 1, has_down & has_right, has_up & has_left),
-        (left_out, low_rows, 1, -1, has_down & has_left, has_up & has_right),
-        (right_out, top_rows, -1, 1, has_up & has_right, has_down & has_left),
-        (left_out, top_rows, -1, -1, has_up & has_left, has_down & has_right),
+    for k, (dr, dc, to, of) in enumerate((
+        (1, 1, has_down & has_right, has_up & has_left),
+        (1, -1, has_down & has_left, has_up & has_right),
+        (-1, 1, has_up & has_right, has_down & has_left),
+        (-1, -1, has_up & has_left, has_down & has_right),
     )):
-        copy = remote(src.at[rows], corner_in.at[k], corner_send.at[k], corner_recv.at[k], me_r + dr, me_c + dc)
+        copy = remote(corner_out.at[k], corner_in.at[k], corner_send.at[k], corner_recv.at[k], me_r + dr, me_c + dc)
         corners.append((copy, to, of))
 
     relayed = 3 if n_rows % 2 == 0 and n_rows > 2 and len(up_cuts) > 3 else 0
@@ -300,6 +300,16 @@
     bulk = load(5, pl.ds(EDGE, low - EDGE))
     for b in (0, height // 16 - 1):
         pack_sides(b)
+    sub = lax.broadcasted_iota(jnp.int32, (8, LANES), 0)
+    for k, (src, start, sign) in enumerate(
+        ((right_out, low, -1), (left_out, low, 1), (right_out, 0, -1), (left_out, 0, 1))
+    ):
+        for part in range(EDGE // 8):
+            block = src[start + part * 8 : start + part * 8 + 8, :]
+            line = jnp.where(sub == 0, block, 0.0)
+            for m in range(1, 8):
+                line = line + pltpu.roll(jnp.where(sub == m, block, 0.0), sign * 3 * SIDE * m % LANES, 1)
+            corner_out[k, :, part * LANES : (part + 1) * LANES] = jnp.sum(line, 0, keepdims=True)
     for copy in bulk:
         copy.wait()
 
@@ -333,7 +343,7 @@
     for k, (_, _, of) in enumerate(corners):
         @pl.when(jnp.logical_not(of))
         def _():
-            corner_in[k] = jnp.zeros((EDGE, LANES), F32)
+            corner_in[k] = jnp.zeros((1, EDGE // 8 * LANES), F32)
 
     for slot, _, of, _, _ in peers:
         @pl.when(jnp.logical_not(of))
@@ -446,8 +456,6 @@
     tab_out[:, 0:LANES] = jnp.sum(acc_g, 0, keepdims=True)
 
     send(4)
-    sub = lax.broadcasted_iota(jnp.int32, (8, LANES), 0)
-
     edge_groups, groups = EDGE // 8, height // 8
 
     def shifted(x, following):
@@ -526,8 +534,8 @@
     def _(t):
         finish(t)
 
+    forward(2)
     send(5)
-    forward(2)
 
     @pl.loop(tiles // 2, tiles)
     def _(t):
@@ -566,8 +574,21 @@
                 def _():
                     copy.wait_recv()
 
-            lane = lax.broadcasted_iota(jnp.int32, (EDGE, LANES), 1)
-            packs = [jnp.where(lane >= LANES // 2, corner_in[k], corner_in[k + 1]) for k in (0, 2)]
+            def unpack(k, part):
+                line = jnp.broadcast_to(corner_in[k, :, part * LANES : (part + 1) * LANES], (8, LANES))
+                block = line
+                for m in range(1, 8):
+                    turned = pltpu.roll(line, (1, -1)[k % 2] * 3 * SIDE * m % LANES, 1)
+                    block = jnp.where(sub == m, turned, block)
+                return block
+
+            lane = lax.broadcasted_iota(jnp.int32, (8, LANES), 1)
+            packs = [
+                jnp.concatenate(
+                    [jnp.where(lane >= LANES // 2, unpack(k, part), unpack(k + 1, part)) for part in range(EDGE // 8)], 0
+                )
+                for k in (0, 2)
+            ]
             for part, pack in enumerate(packs):
                 put_halo(part, decode(*edge_block(pack)), sides)
 
@@ -756,7 +777,8 @@
             pltpu.VMEM((height, LANES), F32),
             pltpu.VMEM((height, LANES), F32),
             pltpu.VMEM((3, EDGE, width), F32),
-            pltpu.VMEM((4, EDGE, LANES), F32),
+            pltpu.VMEM((4, 1, EDGE // 8 * LANES), F32),
+            pltpu.VMEM((4, 1, EDGE // 8 * LANES), F32),
             pltpu.VMEM((2, 4, height, wide), BF16),
             pltpu.VMEM((16 * EDGE, wide), BF16),
             pltpu.VMEM((4, height + 2 * EDGE, width), F32),
@@ -781,7 +803,7 @@
         ),
         name="front",
     )(lead, trail, flags, sweep.reshape(1, height))
-    block = 16 if height % 16 == 0 else 8
+    block = 32 if height % 32 == 0 else 8
     return pl.pallas_call(
         functools.partial(back_kernel, n_rows, n_cols, block),
         out_shape=[

time: 27.4 us -> 27.1 us (0.989)
  the two profiles are of different devices: /device:TPU:19 before, /device:TPU:0 now
where the time goes in v6:
time: 27.1 us; the launch traced here: 26.7 us
  Pallas kernels  26 us (96%)
  between operations  0.64 us (2%)
    pallas_call x1, Pallas kernels, on_device(): pl.pallas_call(functools.partial(front_kernel, n_rows, n_cols, reach), ou...  24.3 us
    pallas_call x1, Pallas kernels, on_device(): pl.pallas_call(functools.partial(back_kernel, n_rows, n_cols, block), out...  1.72 us

profile of v6, /device:TPU:0, one launch (start us, length us, event | category | flops | bytes accessed | tf_op | source)
XLA Modules:
  0.0 26.7 jit_solution(14909650920735050408)
XLA Ops:
  0.6 24.3 %front.1 = (f32[2,128,2048]{2,1,0:T(8,128)S(1)}, f32[128,2048]{1,0:T(8,128)S(1)}, f32[128,128]{1,0:T(8,128)S(1)}, f32[8,128]{1,0:T(8,128)S(1)}) custom-call(f32[2,128,2048]{2,1,0:T(8,128)} %lead.1, f32[2,128,2048]{2,1,0:T(8,128)} %trail.1, s32[128,2048]{1,0:T(8,128)} %flags.1, s32[1,128]{1,0:T(1,128)} %bitcast.1), custom_call_target="tpu_custom_call" | custom-call | tf_op jit(solution)/shard_map/front/pallas_call | solution.py:756
  24.9 1.7 %back.1 = (f32[2,128,2048]{2,1,0:T(8,128)}, f32[128,2048]{1,0:T(8,128)}) custom-call(f32[2,128,2048]{2,1,0:T(8,128)S(1)} %get-tuple-element.6.gam, f32[128,2048]{1,0:T(8,128)S(1)} %get-tuple-element.7.coh, f32[128,128]{1,0:T(8,128)S(1)} %get-tuple-element.8.memt, f32[8,128]{1,0:T(8,128)S(1)} %get-tuple-element.9.fit), custom_call_target="tpu_custom_call" | custom-call | tf_op jit(solution)/shard_map/back/pallas_call | solution.py:807

commit v7 on v6

--- a/solution.py
+++ b/solution.py
@@ -66,7 +66,7 @@
 def cuts(tiles):
     if tiles < EDGE:
         return ((0, tiles),), ((0, tiles),), ((1, 1),)
-    down = [mark * tiles // 16 for mark in (0, 3, 7, 11, 14, 16)]
+    down = [mark * tiles // 16 for mark in (0, 4, 8, 12, 14, 16)]
     up = [mark * tiles // 16 for mark in (0, 5, 9, 13)] + [tiles - 1]
     return tuple(zip(down[:-1], down[1:])), tuple(zip(up[:-1], up[1:])), ((2, 1), (3, 2), (4, 3), (5, 4))
 
@@ -263,7 +263,7 @@
 
     def send(point):
         for v in range(relayed + 1):
-            later = [i for i in range(v, len(down_cuts)) if point == (i + 3 if v else i)]
+            later = [i for i in range(v, len(down_cuts)) if point == (i + (2 if i < 3 else 3) if v else i)]
             for parity, straight, other, asked in ((even, downs, ups, 0), (odd, ups, downs, 1)):
                 ahead = 2 if v == asked == 0 else 1
                 slots = range(ahead + 1) if point == 0 else (point + ahead,)

time: 27.1 us -> 26.6 us (0.982); the launches traced: 26.7 us -> 26.5 us
  no operation moved by 1% of the time
where the time goes in v7:
time: 26.6 us; the launch traced here: 26.5 us
  Pallas kernels  25.8 us (97%)
  between operations  0.64 us (2%)
    pallas_call x1, Pallas kernels, on_device(): pl.pallas_call(functools.partial(front_kernel, n_rows, n_cols, reach), ou...  24.1 us
    pallas_call x1, Pallas kernels, on_device(): pl.pallas_call(functools.partial(back_kernel, n_rows, n_cols, block), out...  1.72 us

profile of v7, /device:TPU:0, one launch (start us, length us, event | category | flops | bytes accessed | tf_op | source)
XLA Modules:
  0.0 26.5 jit_solution(8492070595922976041)
XLA Ops:
  0.6 24.1 %front.1 = (f32[2,128,2048]{2,1,0:T(8,128)S(1)}, f32[128,2048]{1,0:T(8,128)S(1)}, f32[128,128]{1,0:T(8,128)S(1)}, f32[8,128]{1,0:T(8,128)S(1)}) custom-call(f32[2,128,2048]{2,1,0:T(8,128)} %lead.1, f32[2,128,2048]{2,1,0:T(8,128)} %trail.1, s32[128,2048]{1,0:T(8,128)} %flags.1, s32[1,128]{1,0:T(1,128)} %bitcast.1), custom_call_target="tpu_custom_call" | custom-call | tf_op jit(solution)/shard_map/front/pallas_call | solution.py:756
  24.7 1.7 %back.1 = (f32[2,128,2048]{2,1,0:T(8,128)}, f32[128,2048]{1,0:T(8,128)}) custom-call(f32[2,128,2048]{2,1,0:T(8,128)S(1)} %get-tuple-element.6.gam, f32[128,2048]{1,0:T(8,128)S(1)} %get-tuple-element.7.coh, f32[128,128]{1,0:T(8,128)S(1)} %get-tuple-element.8.memt, f32[8,128]{1,0:T(8,128)S(1)} %get-tuple-element.9.fit), custom_call_target="tpu_custom_call" | custom-call | tf_op jit(solution)/shard_map/back/pallas_call | solution.py:807

commit v8 on v7

--- a/solution.py
+++ b/solution.py
@@ -630,7 +630,7 @@
     tab_out[:, LANES:] = jnp.sum(acc_last, 0, keepdims=True)
     swaps = [
         (remote(tab_out, tab_in.at[slot], tab_send.at[slot], tab_recv.at[slot], row, col), to, of)
-        for slot, to, of, row, col in peers
+        for slot, to, of, row, col in sorted(peers, key=lambda p: (p[0] // n_cols == reach, p[0] % n_cols == 0))
     ]
     for copy, to, _ in swaps:
         @pl.when(to)

time: 26.6 us -> 26.6 us (level)
  no operation moved by 1% of the time
where the time goes in v8:
time: 26.6 us; the launch traced here: 26.5 us
  Pallas kernels  25.8 us (97%)
  between operations  0.64 us (2%)
    pallas_call x1, Pallas kernels, on_device(): pl.pallas_call(functools.partial(front_kernel, n_rows, n_cols, reach), ou...  24.1 us
    pallas_call x1, Pallas kernels, on_device(): pl.pallas_call(functools.partial(back_kernel, n_rows, n_cols, block), out...  1.72 us

profile of v8, /device:TPU:0, one launch (start us, length us, event | category | flops | bytes accessed | tf_op | source)
XLA Modules:
  0.0 26.5 jit_solution(13278787731289764934)
XLA Ops:
  0.6 24.1 %front.1 = (f32[2,128,2048]{2,1,0:T(8,128)S(1)}, f32[128,2048]{1,0:T(8,128)S(1)}, f32[128,128]{1,0:T(8,128)S(1)}, f32[8,128]{1,0:T(8,128)S(1)}) custom-call(f32[2,128,2048]{2,1,0:T(8,128)} %lead.1, f32[2,128,2048]{2,1,0:T(8,128)} %trail.1, s32[128,2048]{1,0:T(8,128)} %flags.1, s32[1,128]{1,0:T(1,128)} %bitcast.1), custom_call_target="tpu_custom_call" | custom-call | tf_op jit(solution)/shard_map/front/pallas_call | solution.py:756
  24.8 1.7 %back.1 = (f32[2,128,2048]{2,1,0:T(8,128)}, f32[128,2048]{1,0:T(8,128)}) custom-call(f32[2,128,2048]{2,1,0:T(8,128)S(1)} %get-tuple-element.6.gam, f32[128,2048]{1,0:T(8,128)S(1)} %get-tuple-element.7.coh, f32[128,128]{1,0:T(8,128)S(1)} %get-tuple-element.8.memt, f32[8,128]{1,0:T(8,128)S(1)} %get-tuple-element.9.fit), custom_call_target="tpu_custom_call" | custom-call | tf_op jit(solution)/shard_map/back/pallas_call | solution.py:807
